TPU v7x, 32 devices: a whole 2x2x4 slice. The times are simulated.
32 devices in a mesh: tok: 8 (over y, x, core), blk: 4 (over z).
Axes of the slice: x: 2, y: 2, z: 4, core: 2. Of those that a mesh axis runs over, the one named last changes fastest.
Arguments:
- activations: bfloat16 [4096, 4096], P('tok', 'blk'), may hold values from -52 to 52, as said below
- out_grads: bfloat16 [4096, 4096], P('tok', 'blk'), may hold values from -52 to 52, as said below
Outputs:
- act_inverse: float32 [4096, 4096], P(('tok', 'blk'))
- grad_inverse: float32 [4096, 4096], P(('tok', 'blk'))
Inputs may be any that keep to these rules, and one draw needn't show every extreme that they name: `activations`: real entries. `out_grads`: real entries.
All inputs are finite; a program needn't handle non-finite values.
Results may differ from a plain program's by a relative error of at most 0.02.
Values may be sent and summed in bfloat16 or wider, within the bound.
A program may use at most 64 MiB of HBM per device.

v0:
```python
import functools

import jax
import jax.numpy as jnp
import numpy as np
from jax import lax
from jax.experimental import pallas as pl
from jax.experimental.pallas import tpu as pltpu
from jax.sharding import PartitionSpec as P

damping = 0.3
epsilon = 1e-06
divisor = 2.0
gathered_budget = 32 * 1024 * 1024
LANES = 128
CHUNK = 512
MESH = pl.DeviceIdType.MESH


def column_squares(data):
    values = data.astype(jnp.float32)
    return jnp.sum(values * values, axis=0)


def fold_product(row_block, tile):
    return jnp.dot(
        row_block,
        lax.all_gather(tile, "tok", axis=0, tiled=True),
        preferred_element_type=jnp.float32,
    )


def newton_steps(scaled, identity):
    half = scaled.astype(jnp.bfloat16)
    row_block = lax.all_gather(half, "blk", axis=1, tiled=True)
    square = fold_product(row_block, half)
    cube = fold_product(row_block, square.astype(jnp.bfloat16))
    return 4.0 * identity - 6.0 * scaled + 4.0 * square - cube


def tiled_body(activations, out_grads):
    tok_count = lax.axis_size("tok")
    blk_count = lax.axis_size("blk")
    tok_id = lax.axis_index("tok")
    blk_id = lax.axis_index("blk")
    token_count = activations.shape[0] * tok_count
    tile_cols = activations.shape[1]
    tile_rows = tile_cols * blk_count // tok_count
    row_ids = tok_id * tile_rows + jnp.arange(tile_rows, dtype=jnp.int32)
    col_ids = blk_id * tile_cols + jnp.arange(tile_cols, dtype=jnp.int32)
    identity = (row_ids[:, None] == col_ids[None, :]).astype(jnp.float32)

    def inverse_tile(local):
        full = lax.all_gather(local, "blk", axis=1, tiled=True)
        sums = lax.psum(column_squares(full).astype(jnp.bfloat16), "tok").astype(jnp.float32)
        gram_tile = lax.psum_scatter(
            lax.dot_general(
                full, local, (((0,), (0,)), ((), ())), preferred_element_type=jnp.float32
            ).astype(jnp.bfloat16),
            "tok",
            scatter_dimension=0,
            tiled=True,
        ).astype(jnp.float32)
        inverse = lax.rsqrt(sums / token_count + epsilon)
        inverse_rows = lax.dynamic_slice_in_dim(inverse, tok_id * tile_rows, tile_rows)
        inverse_cols = lax.dynamic_slice_in_dim(inverse, blk_id * tile_cols, tile_cols)
        damped = (
            gram_tile / token_count * inverse_rows[:, None] * inverse_cols[None, :]
            + damping * identity
        )
        result_tile = newton_steps(damped / divisor, identity)
        return lax.all_to_all(
            result_tile.astype(jnp.bfloat16), "blk", split_axis=0, concat_axis=1, tiled=True
        ).astype(result_tile.dtype)

    return inverse_tile(activations), inverse_tile(out_grads)


def cut(length, unit, pieces):
    units = length // unit
    sizes = [(units // pieces + (1 if i < units % pieces else 0)) * unit for i in range(pieces)]
    return [(sum(sizes[:i]), sizes[i]) for i in range(pieces)]


def swap_cut(length, unit, count):
    loads = np.full(count, (2.0**count - 0.5) / count)
    loads[-1] -= 0.5
    steps = np.array([[2.0 ** ((d - j) % count) for j in range(count)] for d in range(count)])
    ends = np.rint(np.cumsum(np.linalg.solve(steps, loads)) * (length // unit)).astype(int) * unit
    ends = [0] + [int(e) for e in ends]
    return [(a, e - a) for a, e in zip(ends, ends[1:])]


def gather_blocks(tok, blk, swaps, first, second, out, sems, halfway=None):
    send_sem, recv_sem, pass_send, pass_recv, swap_send, swap_recv, local_sem = sems
    t = lax.axis_index("tok")
    b = lax.axis_index("blk")
    half = blk // 2
    dims = []
    bit = 2
    while bit < tok:
        dims.append((bit, 0))
        bit *= 2
    bit = 1
    while bit < half:
        dims.append((0, bit))
        bit *= 2
    count = len(dims)
    rows, cols = first.shape
    if swaps:
        parts = [((o, n), (0, cols)) for o, n in (swap_cut if half > 1 else cut)(rows, 16, count)]
    else:
        parts = [((0, rows), (o, n)) for o, n in cut(cols, 128, count)]

    def flip(j, steps, tok_bits=0, blk_bits=0):
        for s in range(count):
            if steps >> s & 1:
                dt, db = dims[(j + s) % count]
                tok_bits ^= dt
                blk_bits ^= db
        return jnp.bitwise_xor(t, tok_bits), jnp.bitwise_xor(b, blk_bits)

    def place(q, part, owner):
        (r0, rn), (c0, cn) = parts[part]
        tt, bb = owner
        if q:
            bb = jnp.bitwise_xor(bb, half)
        if swaps:
            row, col = tt * rows + r0, bb * cols + c0
        else:
            row, col = (tt * blk + bb) * rows + r0, c0
        return out.at[
            pl.ds(pl.multiple_of(row, 16), rn), pl.ds(pl.multiple_of(col, 128), cn)
        ]

    def own(q, part):
        (r0, rn), (c0, cn) = parts[part]
        if q and swaps:
            return place(q, part, (t, b))
        return (second if q else first).at[pl.ds(r0, rn), pl.ds(c0, cn)]

    def hop(q, j, steps, s):
        src = own(q, j) if steps == 0 else place(q, j, flip(j, steps))
        index = (q * count + j) * 2**count + (steps | 1 << s)
        return pltpu.make_async_remote_copy(
            src_ref=src,
            dst_ref=place(q, j, flip(j, steps)),
            send_sem=send_sem.at[index],
            recv_sem=recv_sem.at[index],
            device_id=flip(j, 1 << s),
            device_id_type=MESH,
        )

    def arrival(q, j, steps):
        index = (q * count + j) * 2**count + steps
        where = place(q, j, flip(j, steps))
        return pltpu.make_async_remote_copy(
            src_ref=where,
            dst_ref=where,
            send_sem=send_sem.at[index],
            recv_sem=recv_sem.at[index],
            device_id=flip(j, 1),
            device_id_type=MESH,
        )

    def handed(q, j, steps, sender):
        index = (q * count + j) * 2**count + steps
        if sender:
            where = place(q, j, flip(j, steps))
            src = own(q, j) if steps == 0 else where
        else:
            where = place(q, j, flip(j, steps, 1))
            src = where
        return pltpu.make_async_remote_copy(
            src_ref=src,
            dst_ref=where,
            send_sem=pass_send.at[index],
            recv_sem=pass_recv.at[index],
            device_id=(jnp.bitwise_xor(t, 1), b),
            device_id_type=MESH,
        )

    across = (t, jnp.bitwise_xor(b, half))

    def swap(part, sender):
        (r0, rn), (c0, cn) = parts[part]
        if sender:
            src = second.at[pl.ds(r0, rn), pl.ds(c0, cn)]
            where = place(1, part, across)
        else:
            src = where = place(1, part, (t, b))
        return pltpu.make_async_remote_copy(
            src_ref=src,
            dst_ref=where,
            send_sem=swap_send.at[part],
            recv_sem=swap_recv.at[part],
            device_id=across,
            device_id_type=MESH,
        )

    barrier = pltpu.get_barrier_semaphore()
    peers = [flip(0, 1 << s) for s in range(count)] + [(jnp.bitwise_xor(t, 1), b), across]
    for peer in peers:
        pl.semaphore_signal(barrier, inc=1, device_id=peer, device_id_type=MESH)
    pl.semaphore_wait(barrier, len(peers))

    pending = []

    def start(copy):
        copy.start()
        pending.append(copy)

    def begin(q):
        for s in range(count):
            for j in range(count):
                if s == 0 and q and swaps:
                    swap(j, False).wait_recv()
                start(hop(q, j, 0, s))
        for j in range(count):
            start(handed(q, j, 0, True))

    def advance(q, p):
        for steps in range(2**p, 2 ** (p + 1)):
            for j in range(count):
                arrival(q, j, steps).wait_recv()
                for s in range(p + 1, count):
                    start(hop(q, j, steps, s))
                start(handed(q, j, steps, True))

    begin(0)
    if swaps:
        for part in range(count):
            start(swap(part, True))
    locals_ = []
    for q in range(1 if swaps else 2):
        for part in range(count):
            copy = pltpu.make_async_copy(
                own(q, part), place(q, part, (t, b)), local_sem.at[q * count + part]
            )
            copy.start()
            locals_.append(copy)
    for p in range(count - 1):
        advance(0, p)
    begin(1)
    advance(0, count - 1)
    for copy in locals_:
        copy.wait()

    def received(q):
        for j in range(count):
            for steps in range(2**count):
                handed(q, j, steps, False).wait_recv()

    if halfway is not None:
        received(0)
        halfway()
    for p in range(count):
        advance(1, p)
    if halfway is None:
        received(0)
    received(1)
    for copy in pending:
        copy.wait_send()


def gather_scratch(tok, blk):
    count = (tok // 2).bit_length() - 1 + (blk // 2).bit_length() - 1
    slots = 2 * count * 2**count
    return (
        [pltpu.SemaphoreType.DMA((slots,))] * 4
        + [pltpu.SemaphoreType.DMA((count,))] * 2
        + [pltpu.SemaphoreType.DMA((2 * count,))]
    )


def row_starts(tok, blk, rows):
    t = lax.axis_index("tok")
    b = lax.axis_index("blk")
    return [
        pl.multiple_of((t * blk + bb) * rows, LANES) for bb in (b, jnp.bitwise_xor(b, blk // 2))
    ]


def gram_kernel(tok, blk, first, second, gram, rounded, x, turned, *sems):
    tokens, width = x.shape
    rows = width // (tok * blk)
    gather_blocks(tok, blk, True, first, second, x, sems)
    step = first.shape[0]
    for s, start in enumerate(row_starts(tok, blk, rows)):

        @pl.loop(0, tokens // step)
        def _(i):
            at = pl.ds(pl.multiple_of(i * step, step), step)
            turned[s * rows : (s + 1) * rows, at] = x[at, pl.ds(start, rows)].T

    @pl.loop(0, width // CHUNK)
    def _(i):
        at = pl.ds(pl.multiple_of(i * CHUNK, CHUNK), CHUNK)
        product = jnp.dot(turned[...], x[:, at], preferred_element_type=jnp.float32)
        gram[:, at] = product
        rounded[:, at] = product.astype(jnp.bfloat16)


def newton_kernel(
    tok, blk, tokens, rounded, gram, kept, came, g, square, left, inverse, sent,
    out_sem, in_sem, *sems
):
    width = g.shape[1]
    rows = width // (tok * blk)
    t = lax.axis_index("tok")
    b = lax.axis_index("blk")
    starts = row_starts(tok, blk, rows)
    factor = 1.0 / (tokens * divisor)
    shift = damping / divisor
    eye = lax.broadcasted_iota(jnp.int32, (LANES, LANES), 0) == lax.broadcasted_iota(
        jnp.int32, (LANES, LANES), 1
    )

    inverse_rows = []
    for s, start in enumerate(starts):
        parts = []
        for r in range(0, rows, LANES):
            own = gram[s * rows + r : s * rows + r + LANES, pl.ds(start + r, LANES)]
            total = jnp.sum(jnp.where(eye, own, 0.0), axis=1, keepdims=True)
            parts.append(lax.rsqrt(total / tokens + epsilon))
        inverse_rows += parts
    inverse_rows = jnp.concatenate(inverse_rows, axis=0)

    def identity(first_col, size):
        col = first_col + lax.broadcasted_iota(jnp.int32, (rows, size), 1)
        row = lax.broadcasted_iota(jnp.int32, (rows, size), 0)
        return jnp.concatenate(
            [(col - start == row).astype(jnp.float32) for start in starts], axis=0
        )

    def scaled(first_col, size):
        at = pl.ds(first_col, size)
        return gram[:, at] * factor * inverse_rows * inverse[:, at] + shift * identity(
            first_col, size
        )

    half = blk // 2
    depth = half * rows

    def fold(side, add):
        places = [pl.multiple_of((i * blk + side * half) * rows, LANES) for i in range(tok)]
        for place in places:
            for r in range(0, depth, LANES):
                at = pl.ds(place + r, LANES)
                block = jnp.where(eye, g[at, at].astype(jnp.float32), 0.0)
                total = jnp.sum(block, axis=0, keepdims=True)
                inverse[:, at] = lax.rsqrt(total / tokens + epsilon)
            at = pl.ds(place, depth)
            left[:, at] = (scaled(place, depth) * inverse[:, at]).astype(jnp.bfloat16)

        @pl.loop(0, width // CHUNK)
        def _(i):
            at = pl.ds(pl.multiple_of(i * CHUNK, CHUNK), CHUNK)
            total = square[:, at] if add else jnp.zeros((2 * rows, CHUNK), jnp.float32)
            for place in places:
                deep = pl.ds(place, depth)
                total += jnp.dot(left[:, deep], g[deep, at], preferred_element_type=jnp.float32)
            square[:, at] = total

    side = b // half
    gather_blocks(
        tok, blk, False, rounded.at[pl.ds(0, rows)], rounded.at[pl.ds(rows, rows)], g, sems,
        lambda: fold(side, False),
    )
    fold(1 - side, True)

    @pl.loop(0, width // CHUNK)
    def _(i):
        start = pl.multiple_of(i * CHUNK, CHUNK)
        at = pl.ds(start, CHUNK)
        square[:, at] = square[:, at] * (inverse[:, at] * factor) + shift * scaled(start, CHUNK)
        left[:, at] = (square[:, at] * inverse[:, at]).astype(jnp.bfloat16)

    def swap(i):
        at = pl.ds(pl.multiple_of(i * CHUNK, CHUNK), CHUNK)
        return pltpu.make_async_remote_copy(
            src_ref=sent.at[:, at],
            dst_ref=came.at[:, at],
            send_sem=out_sem.at[i],
            recv_sem=in_sem.at[i],
            device_id=(t, jnp.bitwise_xor(b, blk // 2)),
            device_id_type=MESH,
        )

    steps = width // CHUNK

    def finish(i):
        at = pl.ds(pl.multiple_of(i * CHUNK, CHUNK), CHUNK)
        product = jnp.dot(left[...], g[:, at], preferred_element_type=jnp.float32)
        squared = square[:, at]
        cube = product * (inverse[:, at] * factor) + shift * squared
        start = pl.multiple_of(i * CHUNK, CHUNK)
        result = 4.0 * identity(start, CHUNK) - 6.0 * scaled(start, CHUNK) + 4.0 * squared - cube
        kept[:, at] = result[:rows]
        sent[:, at] = result[rows:].astype(jnp.bfloat16)

    finish(0)

    @pl.loop(1, steps)
    def _(i):
        finish(i)
        swap(i - 1).start()

    swap(steps - 1).start()

    @pl.loop(0, steps)
    def _(i):
        swap(i).wait_recv()
        swap(i).wait_send()


def call(kernel, outs, scratch, tok, blk, collective_id, *operands):
    return pl.pallas_call(
        kernel,
        out_shape=outs,
        in_specs=[pl.BlockSpec(memory_space=pltpu.VMEM)] * len(operands),
        out_specs=[pl.BlockSpec(memory_space=pltpu.VMEM)] * len(outs),
        scratch_shapes=scratch + gather_scratch(tok, blk),
        compiler_params=pltpu.CompilerParams(
            collective_id=collective_id, has_side_effects=True, vmem_limit_bytes=60 * 1024 * 1024
        ),
    )(*operands)


def split_body(tok, blk, activations, out_grads):
    tokens = activations.shape[0] * tok
    width = activations.shape[1] * blk
    rows = width // (tok * blk)
    low = lax.axis_index("blk") < blk // 2
    mine = jnp.where(low, activations, out_grads)
    other = jnp.where(low, out_grads, activations)
    steps = width // CHUNK
    gram, rounded = call(
        functools.partial(gram_kernel, tok, blk),
        [
            jax.ShapeDtypeStruct((2 * rows, width), jnp.float32),
            jax.ShapeDtypeStruct((2 * rows, width), jnp.bfloat16),
        ],
        [
            pltpu.VMEM((tokens, width), jnp.bfloat16),
            pltpu.VMEM((2 * rows, tokens), jnp.bfloat16),
        ],
        tok, blk, 0, mine, other,
    )
    kept, came = call(
        functools.partial(newton_kernel, tok, blk, tokens),
        [
            jax.ShapeDtypeStruct((rows, width), jnp.float32),
            jax.ShapeDtypeStruct((rows, width), jnp.bfloat16),
        ],
        [
            pltpu.VMEM((width, width), jnp.bfloat16),
            pltpu.VMEM((2 * rows, width), jnp.float32),
            pltpu.VMEM((2 * rows, width), jnp.bfloat16),
            pltpu.VMEM((1, width), jnp.float32),
            pltpu.VMEM((rows, width), jnp.bfloat16),
            pltpu.SemaphoreType.DMA((steps,)),
            pltpu.SemaphoreType.DMA((steps,)),
        ],
        tok, blk, 1, rounded, gram,
    )
    came = came.astype(jnp.float32)
    return jnp.where(low, kept, came), jnp.where(low, came, kept)


def solution(mesh):
    tok, blk = mesh.shape["tok"], mesh.shape["blk"]
    placed = (P("tok", "blk"), P("tok", "blk"))

    def body(activations, out_grads):
        tokens, width = activations.shape[0] * tok, activations.shape[1] * blk
        whole = max(tokens, width) * width * activations.dtype.itemsize
        powers = tok & (tok - 1) == 0 and blk & (blk - 1) == 0 and tok > 2 and blk > 1
        powers = powers and width % (tok * blk * LANES) == 0
        if whole <= gathered_budget and powers:
            return split_body(tok, blk, activations, out_grads)
        return tiled_body(activations, out_grads)

    return jax.shard_map(
        body,
        mesh=mesh,
        in_specs=placed,
        out_specs=(P(("tok", "blk"), None), P(("tok", "blk"), None)),
        check_vma=False,
    )
```

profile of v0, /device:TPU:1, one launch (start us, length us, event | category | flops | bytes accessed | tf_op | source)
XLA Modules:
  0.0 337.5 jit_solution(3943471684410277074)
XLA Ops:
  0.6 3.0 broadcast_select_fusion
  3.6 151.7 %shard_map.41 = (f32[256,4096]{1,0:T(8,128)}, bf16[256,4096]{1,0:T(8,128)(2,1)}) custom-call(bf16[512,1024]{1,0:T(8,128)(2,1)} %get-tuple-element.13.first, bf16[512,1024]{1,0:T(8,128)(2,1)} %get-tuple-element.12.second), custom_call_target="tpu_custom_call" | custom-call | tf_op jit(solution)/shard_map/pallas_call | solution.py:418
  155.4 177.8 %shard_map.42 = (f32[128,4096]{1,0:T(8,128)}, bf16[128,4096]{1,0:T(8,128)(2,1)}) custom-call(bf16[256,4096]{1,0:T(8,128)(2,1)} %get-tuple-element.6.rounded, f32[256,4096]{1,0:T(8,128)} %get-tuple-element.7.gram), custom_call_target="tpu_custom_call" | custom-call | tf_op jit(solution)/shard_map/pallas_call | solution.py:418
  333.2 4.4 %convert_select_fusion = (f32[128,4096]{1,0:T(8,128)}, f32[128,4096]{1,0:T(8,128)}) fusion(f32[128,4096]{1,0:T(8,128)} %get-tuple-element.8, bf16[128,4096]{1,0:T(8,128)(2,1)} %get-tuple-element.9, pred[]{:T(512)S(6)} %lt.3), kind=kLoop, calls=%fused_computation | loop fusion | flops 1572864 | bytes 7340033 | tf_op jit(solution)/shard_map/jit(_where)/select_n | solution.py:468
where the time goes:
time: 338 us
  Pallas kernels  330 us (98%)
  other arithmetic  7.37 us (2%)
    pallas_call x2, Pallas kernels, call(): pl.pallas_call(kernel, out_shape=outs, in_specs=[pl.BlockSpec(memory_spac...  330 us

commit v1 on v0

v1 whole, which is shorter than its diff:
```python
import functools

import jax
import jax.numpy as jnp
import numpy as np
from jax import lax
from jax.experimental import pallas as pl
from jax.experimental.pallas import tpu as pltpu
from jax.sharding import PartitionSpec as P

damping = 0.3
epsilon = 1e-06
divisor = 2.0
gathered_budget = 32 * 1024 * 1024
LANES = 128
MESH = pl.DeviceIdType.MESH


def column_squares(data):
    values = data.astype(jnp.float32)
    return jnp.sum(values * values, axis=0)


def fold_product(row_block, tile):
    return jnp.dot(
        row_block,
        lax.all_gather(tile, "tok", axis=0, tiled=True),
        preferred_element_type=jnp.float32,
    )


def newton_steps(scaled, identity):
    half = scaled.astype(jnp.bfloat16)
    row_block = lax.all_gather(half, "blk", axis=1, tiled=True)
    square = fold_product(row_block, half)
    cube = fold_product(row_block, square.astype(jnp.bfloat16))
    return 4.0 * identity - 6.0 * scaled + 4.0 * square - cube


def tiled_body(activations, out_grads):
    tok_count = lax.axis_size("tok")
    blk_count = lax.axis_size("blk")
    tok_id = lax.axis_index("tok")
    blk_id = lax.axis_index("blk")
    token_count = activations.shape[0] * tok_count
    tile_cols = activations.shape[1]
    tile_rows = tile_cols * blk_count // tok_count
    row_ids = tok_id * tile_rows + jnp.arange(tile_rows, dtype=jnp.int32)
    col_ids = blk_id * tile_cols + jnp.arange(tile_cols, dtype=jnp.int32)
    identity = (row_ids[:, None] == col_ids[None, :]).astype(jnp.float32)

    def inverse_tile(local):
        full = lax.all_gather(local, "blk", axis=1, tiled=True)
        sums = lax.psum(column_squares(full).astype(jnp.bfloat16), "tok").astype(jnp.float32)
        gram_tile = lax.psum_scatter(
            lax.dot_general(
                full, local, (((0,), (0,)), ((), ())), preferred_element_type=jnp.float32
            ).astype(jnp.bfloat16),
            "tok",
            scatter_dimension=0,
            tiled=True,
        ).astype(jnp.float32)
        inverse = lax.rsqrt(sums / token_count + epsilon)
        inverse_rows = lax.dynamic_slice_in_dim(inverse, tok_id * tile_rows, tile_rows)
        inverse_cols = lax.dynamic_slice_in_dim(inverse, blk_id * tile_cols, tile_cols)
        damped = (
            gram_tile / token_count * inverse_rows[:, None] * inverse_cols[None, :]
            + damping * identity
        )
        result_tile = newton_steps(damped / divisor, identity)
        return lax.all_to_all(
            result_tile.astype(jnp.bfloat16), "blk", split_axis=0, concat_axis=1, tiled=True
        ).astype(result_tile.dtype)

    return inverse_tile(activations), inverse_tile(out_grads)


DIRECT = {
    (0, 0): (0, 0), (0, 1): (0, 1), (0, 3): (0, 2), (1, 3): (0, 3), (3, 3): (0, 4),
    (1, 1): (1, 0), (1, 2): (1, 1), (2, 0): (1, 2), (2, 3): (1, 3), (2, 2): (1, 4),
}
TASKS = 5
CUTS = 4
LAG = 4


def pick(index, values):
    out = values[-1]
    for i in range(len(values) - 2, -1, -1):
        out = jnp.where(index == i, values[i], out)
    return out


def remote(src, dst, send, recv, device):
    return pltpu.make_async_remote_copy(
        src_ref=src, dst_ref=dst, send_sem=send, recv_sem=recv,
        device_id=device, device_id_type=MESH,
    )


def meet(peers):
    barrier = pltpu.get_barrier_semaphore()
    for peer in peers:
        pl.semaphore_signal(barrier, inc=1, device_id=peer, device_id_type=MESH)
    pl.semaphore_wait(barrier, len(peers))


def gram_kernel(
    tok, blk, acts, grads, out,
    x, other, passed, turned, part, first_in, second_out, second_in, keep,
    load_sem, near_send, near_recv, pass_send, pass_recv, core_send, core_recv,
    one_send, one_recv, two_send, two_recv,
):
    t = lax.axis_index("tok")
    b = lax.axis_index("blk")
    low = b < blk // 2
    place = jnp.where(low, b, blk - 1 - b)
    outer = place == 0
    inner = place == 1
    core, col, row = t % 2, t // 2 % 2, t // 4
    mate = (jnp.bitwise_xor(t, 1), b)
    beside = (jnp.bitwise_xor(t, 2), b)
    below = (jnp.bitwise_xor(t, 4), b)
    near = (t, jnp.bitwise_xor(b, 1))
    facing = (t, blk - 1 - b)
    depth, feats = other.shape
    wide = feats // CUTS
    halfway = feats // 2
    count = TASKS * CUTS

    def load(ref, dst, index):
        return pltpu.make_async_copy(ref, dst, load_sem.at[index])

    @pl.when(low)
    def _():
        load(acts, x.at[place, core], 0).start()
        load(grads, other, 1).start()

    @pl.when(jnp.logical_not(low))
    def _():
        load(grads, x.at[place, core], 0).start()
        load(acts, other, 1).start()

    meet([mate, beside, below, near, facing])
    load(acts, x.at[place, core], 0).wait()
    load(grads, other, 1).wait()

    def columns(h):
        return pl.ds(h * wide, wide)

    def to_mate(label, h):
        here = x.at[label, core, :, columns(h)]
        return remote(
            here, here, core_send.at[label, h], core_recv.at[label, h], mate
        )

    def from_mate(label, h):
        there = x.at[label, 1 - core, :, columns(h)]
        return remote(
            there, there, core_send.at[label, h], core_recv.at[label, h], mate
        )

    def along(label, h, src, device):
        return remote(
            src, x.at[label, core, :, columns(h)],
            near_send.at[label, h], near_recv.at[label, h], device,
        )

    def arrived(label, h):
        here = x.at[label, core, :, columns(h)]
        return remote(here, here, near_send.at[label, h], near_recv.at[label, h], near)

    def give(h):
        return remote(
            other.at[:, columns(h)], passed.at[:, columns(h)],
            pass_send.at[h], pass_recv.at[h], near,
        )

    def onward(h):
        return remote(
            passed.at[:, columns(h)], x.at[3, core, :, columns(h)],
            pass_send.at[h], near_recv.at[3, h], facing,
        )

    for h in range(CUTS):
        to_mate(place, h).start()

    @pl.when(outer)
    def _():
        for h in range(CUTS):
            give(h).start()
        for h in range(CUTS):
            along(0, h, x.at[0, core, :, columns(h)], near).start()

    @pl.when(inner)
    def _():
        for h in range(CUTS):
            along(1, h, x.at[1, core, :, columns(h)], near).start()
            along(2, h, other.at[:, columns(h)], facing).start()

    def turn(slot, label):
        for c in range(2):
            for r in range(0, depth, 256):
                turned[slot, :, c * depth + r : c * depth + r + 256] = x[
                    label, c, r : r + 256, pl.ds(pl.multiple_of(core * halfway, LANES), halfway)
                ].T

    def share(label, h):
        arrived(label, h).wait_recv()
        to_mate(label, h).start()

    def piece(n):
        late = n - jnp.where(outer, 2, 3) * CUTS
        pairs = late // 2
        paired = jnp.where(outer, (n >= 2 * CUTS) & (n < 4 * CUTS), n >= 3 * CUTS)
        task = jnp.where(paired, 2 + late % 2, jnp.where(n < 2 * CUTS, n // CUTS, 4))
        h = jnp.where(paired, pairs, n % CUTS)
        slot = jnp.where(outer, pick(task, [0, 0, 0, 1, 2]), pick(task, [0, 0, 1, 1, 1]))
        label = jnp.where(outer, pick(task, [0, 1, 3, 3, 3]), pick(task, [1, 2, 0, 3, 2]))
        return task, h, slot, label

    def one(n, side):
        if side == 0:
            src, device = part.at[n, :, 1 - col, :, pl.ds(0, wide // 2)], beside
        else:
            src, device = part.at[n, 1 - row, :, :, pl.ds(wide // 2, wide // 2)], below
        return remote(
            src, first_in.at[n, side], one_send.at[n, side], one_recv.at[n, side], device
        )

    def two(n, side):
        return remote(
            second_out.at[n, side], second_in.at[n, side],
            two_send.at[n, side], two_recv.at[n, side], below if side == 0 else beside,
        )

    for h in range(CUTS):
        from_mate(place, h).wait_recv()
    turn(0, place)

    @pl.loop(0, count + 2 * LAG)
    def _(n):
        @pl.when(n == CUTS)
        def _():
            @pl.when(inner)
            def _():
                for h in range(CUTS):
                    give(h).wait_recv()
                    onward(h).start()

            label = place + 1
            for h in range(CUTS):
                share(label, h)
            for h in range(CUTS):
                from_mate(label, h).wait_recv()
            turn(1, label)

        late = n - jnp.where(outer, 2, 3) * CUTS
        paired = jnp.where(outer, (n >= 2 * CUTS) & (n < 4 * CUTS), n >= 3 * CUTS)

        @pl.when(paired & (late % 2 == 0) & (n < count))
        def _():
            h = late // 2
            arrived(3, h).wait_recv()
            to_mate(3, h).start()

            @pl.when(inner)
            def _():
                along(3, h, x.at[3, core, :, columns(h)], near).start()
                share(0, h)
                from_mate(0, h).wait_recv()

            from_mate(3, h).wait_recv()

        @pl.when(outer & (n == 4 * CUTS))
        def _():
            turn(2, 3)

        @pl.when(n < count)
        def _():
            task, h, slot, label = piece(n)
            at = pl.ds(pl.multiple_of(h * wide, LANES), wide)
            right = x[label, :, :, at].reshape(2 * depth, wide)
            product = jnp.dot(turned[slot], right, preferred_element_type=jnp.float32)
            part[n] = product.astype(jnp.bfloat16).reshape(2, 2, LANES, wide)
            one(n, 0).start()
            one(n, 1).start()

        @pl.when((n >= LAG) & (n < count + LAG))
        def _():
            m = n - LAG
            left, right = pl.ds(0, wide // 2), pl.ds(wide // 2, wide // 2)
            one(m, 0).wait_recv()
            one(m, 1).wait_recv()
            wider = jnp.float32
            second_out[m, 0] = (
                part[m, 1 - row, col, :, left].astype(wider)
                + first_in[m, 0, 1 - row].astype(wider)
            ).astype(jnp.bfloat16)
            second_out[m, 1] = (
                part[m, row, 1 - col, :, right].astype(wider)
                + first_in[m, 1, 1 - col].astype(wider)
            ).astype(jnp.bfloat16)
            two(m, 0).start()
            two(m, 1).start()
            keep[m, 0] = part[m, row, col, :, left].astype(wider) + first_in[
                m, 0, row
            ].astype(wider)
            keep[m, 1] = part[m, row, col, :, right].astype(wider) + first_in[
                m, 1, col
            ].astype(wider)

        @pl.when(n >= 2 * LAG)
        def _():
            m = n - 2 * LAG
            task, h, _, _ = piece(m)
            two(m, 0).wait_recv()
            two(m, 1).wait_recv()
            rows = pl.ds(pl.multiple_of(task * LANES, LANES), LANES)
            for side in range(2):
                at = pl.ds(pl.multiple_of(h * wide + side * (wide // 2), LANES), wide // 2)
                total = keep[m, side] + second_in[m, side].astype(jnp.float32)
                out[rows, at] = total.astype(jnp.bfloat16)

    @pl.loop(0, count)
    def _(n):
        for side in range(2):
            one(n, side).wait_send()
            two(n, side).wait_send()

    for h in range(CUTS):
        to_mate(place, h).wait_send()
        to_mate(place + 1, h).wait_send()
        to_mate(3, h).wait_send()

    @pl.when(outer)
    def _():
        for h in range(CUTS):
            give(h).wait_send()
            along(0, h, x.at[0, core, :, columns(h)], near).wait_send()

    @pl.when(inner)
    def _():
        for h in range(CUTS):
            along(1, h, x.at[1, core, :, columns(h)], near).wait_send()
            along(2, h, other.at[:, columns(h)], facing).wait_send()
            along(3, h, x.at[3, core, :, columns(h)], near).wait_send()
            onward(h).wait_send()
            to_mate(0, h).wait_send()


def newton_kernel(
    tok, blk, tokens, mine, kept, came, g, mixed, square, left, inverse, sent,
    send_sem, recv_sem, pass_send, pass_recv, local_sem, out_sem, in_sem,
):
    t = lax.axis_index("tok")
    b = lax.axis_index("blk")
    low = b < blk // 2
    half = blk // 2
    feats = g.shape[2]
    owners = g.shape[0]
    width = square.shape[1]
    labels = width // feats
    rows = LANES
    factor = 1.0 / (tokens * divisor)
    shift = damping / divisor
    dims = [(2, 0), (4, 0), (0, 1)]
    count = len(dims)

    def owner(device):
        tt, bb = device
        place = jnp.where(low, bb, blk - 1 - bb)
        return place * (owners // 2) + tt % 2 * (owners // 4) + tt // 2

    height = mine.shape[0]
    groups = cut(height, 16, 2)
    parts = [[(o + a, n) for a, n in cut(size, 16, count)] for o, size in groups]

    def flip(j, steps, tok_bits=0):
        blk_bits = 0
        for s in range(count):
            if steps >> s & 1:
                dt, db = dims[(j + s) % count]
                tok_bits ^= dt
                blk_bits ^= db
        return jnp.bitwise_xor(t, tok_bits), jnp.bitwise_xor(b, blk_bits)

    def spot(q, j, device):
        o, n = parts[q][j]
        return g.at[owner(device), pl.ds(o, n)]

    def own(q, j):
        o, n = parts[q][j]
        return mine.at[pl.ds(o, n)]

    def slot(q, j, steps):
        return (q * count + j) * 2**count + steps

    def hop(q, j, steps, s):
        index = slot(q, j, steps | 1 << s)
        where = spot(q, j, flip(j, steps))
        src = own(q, j) if steps == 0 else where
        return remote(src, where, send_sem.at[index], recv_sem.at[index], flip(j, 1 << s))

    def arrival(q, j, steps):
        index = slot(q, j, steps)
        where = spot(q, j, flip(j, steps))
        return remote(where, where, send_sem.at[index], recv_sem.at[index], flip(j, 1))

    mate = (jnp.bitwise_xor(t, 1), b)
    across = (t, jnp.bitwise_xor(b, half))

    def handed(q, j, steps, sender):
        index = slot(q, j, steps)
        where = spot(q, j, flip(j, steps, 0 if sender else 1))
        src = own(q, j) if sender and steps == 0 else where
        return remote(src, where, pass_send.at[index], pass_recv.at[index], mate)

    meet([flip(0, 1 << s) for s in range(count)] + [mate, across])
    pending = []

    def start(copy):
        copy.start()
        pending.append(copy)

    def begin(q):
        for s in range(count):
            for j in range(count):
                start(hop(q, j, 0, s))
        for j in range(count):
            start(handed(q, j, 0, True))

    def advance(q, p):
        for steps in range(2**p, 2 ** (p + 1)):
            for j in range(count):
                arrival(q, j, steps).wait_recv()
                for s in range(p + 1, count):
                    start(hop(q, j, steps, s))
                start(handed(q, j, steps, True))

    begin(0)
    local = pltpu.make_async_copy(mine, g.at[owner((t, b))], local_sem)
    local.start()
    for p in range(count - 1):
        advance(0, p)
    begin(1)
    advance(0, count - 1)
    for p in range(count):
        advance(1, p)
    local.wait()
    for q in range(len(groups)):
        for j in range(count):
            for steps in range(2**count):
                handed(q, j, steps, False).wait_recv()

    eye = lax.broadcasted_iota(jnp.int32, (LANES, LANES), 0) == lax.broadcasted_iota(
        jnp.int32, (LANES, LANES), 1
    )
    eighth = owners // 2

    def diagonal(o, k, sub, axis):
        at = pl.ds(pl.multiple_of(sub * LANES, LANES), LANES)
        own_rows = pl.ds(pl.multiple_of(k * LANES, LANES), LANES)
        block = jnp.where(eye, g[o, own_rows, at].astype(jnp.float32), 0.0)
        total = jnp.sum(block, axis=axis, keepdims=True)
        return lax.rsqrt(total / tokens + epsilon)

    for label in range(labels):
        place, k = DIRECT[label, label]

        @pl.loop(0, eighth)
        def _(sub):
            at = pl.ds(pl.multiple_of(label * feats + sub * LANES, LANES), LANES)
            inverse[:, at] = diagonal(place * eighth + sub, k, sub, 0)

    block_of_rows = t // 2
    row_label = jnp.where(low, block_of_rows, labels - 1 - block_of_rows)
    subs = [t % 2 * blk + bb for bb in (b, jnp.bitwise_xor(b, half))]
    diag_place = pick(row_label, [DIRECT[i, i][0] for i in range(labels)])
    diag_task = pick(row_label, [DIRECT[i, i][1] for i in range(labels)])
    inverse_rows = jnp.concatenate(
        [diagonal(diag_place * eighth + sub, diag_task, sub, 1) for sub in subs], axis=0
    )

    for label in range(labels):

        @pl.when(row_label == label)
        def _():
            for j in range(labels):
                cols = slice(j * feats, (j + 1) * feats)
                for s, sub in enumerate(subs):
                    if (label, j) in DIRECT:
                        place, k = DIRECT[label, j]
                        value = g[place * eighth + sub, k * LANES : (k + 1) * LANES, :]
                    else:
                        place, k = DIRECT[j, label]
                        at = pl.ds(pl.multiple_of(sub * LANES, LANES), LANES)
                        value = g[
                            place * eighth : (place + 1) * eighth, k * LANES : (k + 1) * LANES, at
                        ]
                        value = value.reshape(feats, LANES).T
                    mixed[s * rows : (s + 1) * rows, cols] = value

    step = feats // CUTS
    starts = [row_label * feats + sub * LANES for sub in subs]

    def identity(first_col, size):
        at = first_col + lax.broadcasted_iota(jnp.int32, (rows, size), 1)
        row = lax.broadcasted_iota(jnp.int32, (rows, size), 0)
        return jnp.concatenate(
            [(at - start == row).astype(jnp.float32) for start in starts], axis=0
        )

    def scaled(first_col, size):
        at = pl.ds(first_col, size)
        return mixed[:, at].astype(jnp.float32) * (
            factor * inverse_rows
        ) * inverse[:, at] + shift * identity(first_col, size)

    def fold(label, h):
        total = None
        for k in range(labels):
            lhs = left[:, k * feats : (k + 1) * feats]
            if (k, label) in DIRECT:
                place, task = DIRECT[k, label]
                rhs = g[
                    place * eighth : (place + 1) * eighth,
                    task * LANES : (task + 1) * LANES,
                    pl.ds(pl.multiple_of(h * step, LANES), step),
                ].reshape(feats, step)
                product = jnp.dot(lhs, rhs, preferred_element_type=jnp.float32)
            else:
                place, task = DIRECT[label, k]
                few = step // LANES
                rhs = g[
                    pl.ds(place * eighth + h * few, few), task * LANES : (task + 1) * LANES, :
                ].reshape(step, feats)
                product = lax.dot_general(
                    lhs, rhs, (((1,), (1,)), ((), ())), preferred_element_type=jnp.float32
                )
            total = product if total is None else total + product
        return total

    @pl.loop(0, labels * CUTS)
    def _(i):
        start_col = pl.multiple_of(i * step, step)
        at = pl.ds(start_col, step)
        left[:, at] = (scaled(start_col, step) * inverse[:, at]).astype(jnp.bfloat16)

    for label in range(labels):

        @pl.loop(0, CUTS)
        def _(h):
            start_col = pl.multiple_of(label * feats + h * step, step)
            at = pl.ds(start_col, step)
            square[:, at] = fold(label, h) * (inverse[:, at] * factor) + shift * scaled(
                start_col, step
            )

    @pl.loop(0, labels * CUTS)
    def _(i):
        start_col = pl.multiple_of(i * step, step)
        at = pl.ds(start_col, step)
        left[:, at] = (square[:, at] * inverse[:, at]).astype(jnp.bfloat16)

    def swap(label, h):
        to = jnp.where(low, label, labels - 1 - label)
        at = pl.ds(pl.multiple_of(to * feats + h * step, LANES), step)
        index = label * CUTS + h
        return at, remote(
            sent.at[:, at], came.at[:, at], out_sem.at[index], in_sem.at[index], across
        )

    for label in range(labels):

        @pl.loop(0, CUTS)
        def _(h):
            start_col = pl.multiple_of(label * feats + h * step, step)
            at = pl.ds(start_col, step)
            squared = square[:, at]
            cube = fold(label, h) * (inverse[:, at] * factor) + shift * squared
            result = (
                4.0 * identity(start_col, step) - 6.0 * scaled(start_col, step)
                + 4.0 * squared - cube
            )
            to, copy = swap(label, h)
            kept[:, to] = result[:rows]
            sent[:, to] = result[rows:].astype(jnp.bfloat16)
            copy.start()

    for label in range(labels):

        @pl.loop(0, CUTS)
        def _(h):
            _, copy = swap(label, h)
            copy.wait_recv()
            copy.wait_send()

    for copy in pending:
        copy.wait_send()


def cut(length, unit, pieces):
    units = length // unit
    sizes = [(units // pieces + (1 if i < units % pieces else 0)) * unit for i in range(pieces)]
    return [(sum(sizes[:i]), sizes[i]) for i in range(pieces)]


def call(kernel, outs, scratch, collective_id, space, *operands):
    return pl.pallas_call(
        kernel,
        out_shape=outs,
        in_specs=[pl.BlockSpec(memory_space=space)] * len(operands),
        out_specs=[pl.BlockSpec(memory_space=pltpu.VMEM)] * len(outs),
        scratch_shapes=scratch,
        compiler_params=pltpu.CompilerParams(
            collective_id=collective_id, has_side_effects=True, vmem_limit_bytes=60 * 1024 * 1024
        ),
    )(*operands)


def split_body(tok, blk, activations, out_grads):
    depth, feats = activations.shape
    tokens = depth * tok
    width = feats * blk
    rows = width // (tok * blk)
    low = lax.axis_index("blk") < blk // 2
    count = TASKS * CUTS
    wide = feats // CUTS
    bf16, f32 = jnp.bfloat16, jnp.float32
    dma = pltpu.SemaphoreType.DMA
    (mine,) = call(
        functools.partial(gram_kernel, tok, blk),
        [jax.ShapeDtypeStruct((TASKS * rows, feats), bf16)],
        [
            pltpu.VMEM((blk, 2, depth, feats), bf16),
            pltpu.VMEM((depth, feats), bf16),
            pltpu.VMEM((depth, feats), bf16),
            pltpu.VMEM((3, feats // 2, 2 * depth), bf16),
            pltpu.VMEM((count, 2, 2, rows, wide), bf16),
            pltpu.VMEM((count, 2, 2, rows, wide // 2), bf16),
            pltpu.VMEM((count, 2, rows, wide // 2), bf16),
            pltpu.VMEM((count, 2, rows, wide // 2), bf16),
            pltpu.VMEM((count, 2, rows, wide // 2), f32),
            dma((2,)),
            dma((blk, CUTS)), dma((blk, CUTS)),
            dma((CUTS,)), dma((CUTS,)),
            dma((blk, CUTS)), dma((blk, CUTS)),
            dma((count, 2)), dma((count, 2)), dma((count, 2)), dma((count, 2)),
        ],
        0, pl.ANY, activations, out_grads,
    )
    slots = 2 * 3 * 8
    steps = blk * CUTS
    kept, came = call(
        functools.partial(newton_kernel, tok, blk, tokens),
        [jax.ShapeDtypeStruct((rows, width), f32), jax.ShapeDtypeStruct((rows, width), bf16)],
        [
            pltpu.VMEM((2 * tok, TASKS * rows, feats), bf16),
            pltpu.VMEM((2 * rows, width), bf16),
            pltpu.VMEM((2 * rows, width), f32),
            pltpu.VMEM((2 * rows, width), bf16),
            pltpu.VMEM((1, width), f32),
            pltpu.VMEM((rows, width), bf16),
            dma((slots,)), dma((slots,)), dma((slots,)), dma((slots,)), dma,
            dma((steps,)), dma((steps,)),
        ],
        1, pltpu.VMEM, mine,
    )
    came = came.astype(f32)
    return jnp.where(low, kept, came), jnp.where(low, came, kept)


def solution(mesh):
    tok, blk = mesh.shape["tok"], mesh.shape["blk"]
    placed = (P("tok", "blk"), P("tok", "blk"))

    def body(activations, out_grads):
        depth, feats = activations.shape
        whole = max(depth * tok, feats * blk) * feats * blk * activations.dtype.itemsize
        cube = tok == 2 * blk and blk == 4 and feats == tok * LANES
        if whole <= gathered_budget and cube:
            return split_body(tok, blk, activations, out_grads)
        return tiled_body(activations, out_grads)

    return jax.shard_map(
        body,
        mesh=mesh,
        in_specs=placed,
        out_specs=(P(("tok", "blk"), None), P(("tok", "blk"), None)),
        check_vma=False,
    )
```

time: 338 us -> 233 us (0.69)
  Pallas kernels: 330 us -> 228 us
    pallas_call x2, Pallas kernels: 330 us -> 228 us  [call(): pl.pallas_call(kernel, out_shape=outs, in_specs=[pl.BlockSpec(memory_spac...]
where the time goes in v1:
time: 233 us
  Pallas kernels  228 us (98%)
  other arithmetic  4.38 us (2%)
    pallas_call x2, Pallas kernels, call(): pl.pallas_call(kernel, out_shape=outs, in_specs=[pl.BlockSpec(memory_spac...  228 us

profile of v1, /device:TPU:1, one launch (start us, length us, event | category | flops | bytes accessed | tf_op | source)
XLA Modules:
  0.0 232.7 jit_solution(13874550776137758632)
XLA Ops:
  0.6 87.2 %shard_map.41.mine = bf16[640,1024]{1,0:T(8,128)(2,1)} custom-call(bf16[512,1024]{1,0:T(8,128)(2,1)} %acts.1, bf16[512,1024]{1,0:T(8,128)(2,1)} %grads.1), custom_call_target="tpu_custom_call" | custom-call | tf_op jit(solution)/shard_map/pallas_call | solution.py:610
  87.9 140.5 %shard_map.42 = (f32[128,4096]{1,0:T(8,128)}, bf16[128,4096]{1,0:T(8,128)(2,1)}) custom-call(bf16[640,1024]{1,0:T(8,128)(2,1)} %shard_map.41.mine), custom_call_target="tpu_custom_call" | custom-call | tf_op jit(solution)/shard_map/pallas_call | solution.py:610
  228.4 4.4 %convert_select_fusion = (f32[128,4096]{1,0:T(8,128)}, f32[128,4096]{1,0:T(8,128)}) fusion(f32[128,4096]{1,0:T(8,128)} %get-tuple-element.4, bf16[128,4096]{1,0:T(8,128)(2,1)} %get-tuple-element.5, pred[]{:T(512)S(6)} %lt.3), kind=kLoop, calls=%fused_computation | loop fusion | flops 1572864 | bytes 7340033 | tf_op jit(solution)/shard_map/jit(_where)/select_n | solution.py:671

commit v2 on v1

--- a/solution.py
+++ b/solution.py
@@ -81,7 +81,8 @@
 }
 TASKS = 5
 CUTS = 4
-LAG = 4
+ADD_LAG = 3
+END_LAG = 6
 
 
 def pick(index, values):
@@ -146,7 +147,7 @@
     load(grads, other, 1).wait()
 
     def columns(h):
-        return pl.ds(h * wide, wide)
+        return pl.ds(pl.multiple_of(h * wide, LANES), wide)
 
     def to_mate(label, h):
         here = x.at[label, core, :, columns(h)]
@@ -238,22 +239,23 @@
         from_mate(place, h).wait_recv()
     turn(0, place)
 
-    @pl.loop(0, count + 2 * LAG)
+    @pl.loop(0, count + END_LAG)
     def _(n):
-        @pl.when(n == CUTS)
-        def _():
+        @pl.when((n >= CUTS) & (n < 2 * CUTS))
+        def _():
+            h = n - CUTS
+
             @pl.when(inner)
             def _():
-                for h in range(CUTS):
-                    give(h).wait_recv()
-                    onward(h).start()
-
-            label = place + 1
-            for h in range(CUTS):
-                share(label, h)
-            for h in range(CUTS):
-                from_mate(label, h).wait_recv()
-            turn(1, label)
+                give(h).wait_recv()
+                onward(h).start()
+
+            share(place + 1, h)
+            from_mate(place + 1, h).wait_recv()
+
+        @pl.when(n == 2 * CUTS)
+        def _():
+            turn(1, place + 1)
 
         late = n - jnp.where(outer, 2, 3) * CUTS
         paired = jnp.where(outer, (n >= 2 * CUTS) & (n < 4 * CUTS), n >= 3 * CUTS)
@@ -286,9 +288,9 @@
             one(n, 0).start()
             one(n, 1).start()
 
-        @pl.when((n >= LAG) & (n < count + LAG))
-        def _():
-            m = n - LAG
+        @pl.when((n >= ADD_LAG) & (n < count + ADD_LAG))
+        def _():
+            m = n - ADD_LAG
             left, right = pl.ds(0, wide // 2), pl.ds(wide // 2, wide // 2)
             one(m, 0).wait_recv()
             one(m, 1).wait_recv()
@@ -310,9 +312,9 @@
                 m, 1, col
             ].astype(wider)
 
-        @pl.when(n >= 2 * LAG)
-        def _():
-            m = n - 2 * LAG
+        @pl.when(n >= END_LAG)
+        def _():
+            m = n - END_LAG
             task, h, _, _ = piece(m)
             two(m, 0).wait_recv()
             two(m, 1).wait_recv()

time: 233 us -> 228 us (0.979)
  Pallas kernels: 228 us -> 223 us
    pallas_call x2, Pallas kernels: 228 us -> 223 us  [call(): pl.pallas_call(kernel, out_shape=outs, in_specs=[pl.BlockSpec(memory_spac...]
where the time goes in v2:
time: 228 us
  Pallas kernels  223 us (98%)
  other arithmetic  4.38 us (2%)
    pallas_call x2, Pallas kernels, call(): pl.pallas_call(kernel, out_shape=outs, in_specs=[pl.BlockSpec(memory_spac...  223 us

profile of v2, /device:TPU:1, one launch (start us, length us, event | category | flops | bytes accessed | tf_op | source)
XLA Modules:
  0.0 227.8 jit_solution(14159886402118769282)
XLA Ops:
  0.6 81.7 %shard_map.41.mine = bf16[640,1024]{1,0:T(8,128)(2,1)} custom-call(bf16[512,1024]{1,0:T(8,128)(2,1)} %acts.1, bf16[512,1024]{1,0:T(8,128)(2,1)} %grads.1), custom_call_target="tpu_custom_call" | custom-call | tf_op jit(solution)/shard_map/pallas_call | solution.py:612
  82.4 141.1 %shard_map.42 = (f32[128,4096]{1,0:T(8,128)}, bf16[128,4096]{1,0:T(8,128)(2,1)}) custom-call(bf16[640,1024]{1,0:T(8,128)(2,1)} %shard_map.41.mine), custom_call_target="tpu_custom_call" | custom-call | tf_op jit(solution)/shard_map/pallas_call | solution.py:612
  223.5 4.4 %convert_select_fusion = (f32[128,4096]{1,0:T(8,128)}, f32[128,4096]{1,0:T(8,128)}) fusion(f32[128,4096]{1,0:T(8,128)} %get-tuple-element.4, bf16[128,4096]{1,0:T(8,128)(2,1)} %get-tuple-element.5, pred[]{:T(512)S(6)} %lt.3), kind=kLoop, calls=%fused_computation | loop fusion | flops 1572864 | bytes 7340033 | tf_op jit(solution)/shard_map/jit(_where)/select_n | solution.py:673

commit v3 on v2

--- a/solution.py
+++ b/solution.py
@@ -80,6 +80,7 @@
     (1, 1): (1, 0), (1, 2): (1, 1), (2, 0): (1, 2), (2, 3): (1, 3), (2, 2): (1, 4),
 }
 TASKS = 5
+EARLY = 2
 CUTS = 4
 ADD_LAG = 3
 END_LAG = 6
@@ -106,11 +107,13 @@
     pl.semaphore_wait(barrier, len(peers))
 
 
-def gram_kernel(
-    tok, blk, acts, grads, out,
+def factor_kernel(
+    tok, blk, tokens, acts, grads, kept, came,
     x, other, passed, turned, part, first_in, second_out, second_in, keep,
+    g, mixed, square, left, inverse, sent,
     load_sem, near_send, near_recv, pass_send, pass_recv, core_send, core_recv,
     one_send, one_recv, two_send, two_recv,
+    hop_send, hop_recv, hand_send, hand_recv, out_sem, in_sem,
 ):
     t = lax.axis_index("tok")
     b = lax.axis_index("blk")
@@ -124,6 +127,7 @@
     below = (jnp.bitwise_xor(t, 4), b)
     near = (t, jnp.bitwise_xor(b, 1))
     facing = (t, blk - 1 - b)
+    across = (t, jnp.bitwise_xor(b, blk // 2))
     depth, feats = other.shape
     wide = feats // CUTS
     halfway = feats // 2
@@ -142,7 +146,7 @@
         load(grads, x.at[place, core], 0).start()
         load(acts, other, 1).start()
 
-    meet([mate, beside, below, near, facing])
+    meet([mate, beside, below, near, facing, across])
     load(acts, x.at[place, core], 0).wait()
     load(grads, other, 1).wait()
 
@@ -211,11 +215,9 @@
         to_mate(label, h).start()
 
     def piece(n):
-        late = n - jnp.where(outer, 2, 3) * CUTS
-        pairs = late // 2
-        paired = jnp.where(outer, (n >= 2 * CUTS) & (n < 4 * CUTS), n >= 3 * CUTS)
-        task = jnp.where(paired, 2 + late % 2, jnp.where(n < 2 * CUTS, n // CUTS, 4))
-        h = jnp.where(paired, pairs, n % CUTS)
+        paired = (n >= 2 * CUTS) & (n < 4 * CUTS)
+        task = jnp.where(paired, 2 + n % 2, jnp.where(n < 2 * CUTS, n // CUTS, 4))
+        h = jnp.where(paired, n // 2 - CUTS, n % CUTS)
         slot = jnp.where(outer, pick(task, [0, 0, 0, 1, 2]), pick(task, [0, 0, 1, 1, 1]))
         label = jnp.where(outer, pick(task, [0, 1, 3, 3, 3]), pick(task, [1, 2, 0, 3, 2]))
         return task, h, slot, label
@@ -235,13 +237,82 @@
             two_send.at[n, side], two_recv.at[n, side], below if side == 0 else beside,
         )
 
+    owners = g.shape[0]
+    eighth = owners // 2
+    orders = [[[0, 1, 2], [1, 0, 2]], [[2, 0, 1], [2, 1, 0]]]
+    moves = [(2, 0), (4, 0), (0, 1)]
+    stages = len(moves)
+    ranges = []
+    for first, last in ((0, EARLY), (EARLY, TASKS)):
+        ranges.append([(first * LANES + o, n) for o, n in cut((last - first) * LANES, 16, 2)])
+
+    def owner(device):
+        tt, bb = device
+        side = jnp.where(low, bb, blk - 1 - bb)
+        return side * eighth + tt % 2 * (eighth // 2) + tt // 2
+
+    me = owner((t, b))
+
+    def flip(q, j, steps, tok_bits=0):
+        blk_bits = 0
+        for s in range(stages):
+            if steps >> s & 1:
+                dt, db = moves[orders[q][j][s]]
+                tok_bits ^= dt
+                blk_bits ^= db
+        return jnp.bitwise_xor(t, tok_bits), jnp.bitwise_xor(b, blk_bits)
+
+    def spot(q, j, device):
+        o, n = ranges[q][j]
+        return g.at[owner(device), pl.ds(o, n)]
+
+    def index_of(q, j, steps):
+        return (q * 2 + j) * 2**stages + steps
+
+    def hop(q, j, steps, s):
+        index = index_of(q, j, steps | 1 << s)
+        where = spot(q, j, flip(q, j, steps))
+        return remote(
+            where, where, hop_send.at[index], hop_recv.at[index], flip(q, j, 1 << s)
+        )
+
+    def arrival(q, j, steps):
+        index = index_of(q, j, steps)
+        where = spot(q, j, flip(q, j, steps))
+        return remote(where, where, hop_send.at[index], hop_recv.at[index], flip(q, j, 1))
+
+    def hand(q, j, steps, sender):
+        index = index_of(q, j, steps)
+        where = spot(q, j, flip(q, j, steps, 0 if sender else 1))
+        return remote(where, where, hand_send.at[index], hand_recv.at[index], mate)
+
+    def every(q, steps, s):
+        for j in range(2):
+            hop(q, j, steps, s).start()
+
+    def landed(q, steps, onward_to=()):
+        for j in range(2):
+            arrival(q, j, steps).wait_recv()
+            for s in onward_to:
+                hop(q, j, steps, s).start()
+            hand(q, j, steps, True).start()
+
     for h in range(CUTS):
         from_mate(place, h).wait_recv()
     turn(0, place)
 
-    @pl.loop(0, count + END_LAG)
-    def _(n):
-        @pl.when((n >= CUTS) & (n < 2 * CUTS))
+    split = 2 * CUTS
+    gap = END_LAG
+
+    def at_step(i):
+        inside = (i >= 0) & ((i < split) | ((i >= split + gap) & (i < count + gap)))
+        return inside, jnp.where(i < split, i, i - gap)
+
+    @pl.loop(0, count + gap + END_LAG)
+    def _(i):
+        active, n = at_step(i)
+
+        @pl.when(active & (n >= CUTS) & (n < split))
         def _():
             h = n - CUTS
 
@@ -253,16 +324,28 @@
             share(place + 1, h)
             from_mate(place + 1, h).wait_recv()
 
-        @pl.when(n == 2 * CUTS)
-        def _():
+        @pl.when(i == split + gap)
+        def _():
+            for s in (0, 1):
+                every(0, 0, s)
+            for j in range(2):
+                hand(0, j, 0, True).start()
             turn(1, place + 1)
 
-        late = n - jnp.where(outer, 2, 3) * CUTS
-        paired = jnp.where(outer, (n >= 2 * CUTS) & (n < 4 * CUTS), n >= 3 * CUTS)
-
-        @pl.when(paired & (late % 2 == 0) & (n < count))
-        def _():
-            h = late // 2
+        @pl.when(i == split + gap + CUTS)
+        def _():
+            landed(0, 1, (1,))
+
+        @pl.when(i == split + gap + 2 * CUTS)
+        def _():
+            landed(0, 2)
+            landed(0, 3)
+            every(0, 0, 2)
+            every(0, 1, 2)
+
+        @pl.when(active & (n >= split) & (n < 2 * split) & (n % 2 == 0))
+        def _():
+            h = n // 2 - CUTS
             arrived(3, h).wait_recv()
             to_mate(3, h).start()
 
@@ -274,11 +357,11 @@
 
             from_mate(3, h).wait_recv()
 
-        @pl.when(outer & (n == 4 * CUTS))
+        @pl.when(outer & (i == 2 * split + gap))
         def _():
             turn(2, 3)
 
-        @pl.when(n < count)
+        @pl.when(active)
         def _():
             task, h, slot, label = piece(n)
             at = pl.ds(pl.multiple_of(h * wide, LANES), wide)
@@ -288,177 +371,73 @@
             one(n, 0).start()
             one(n, 1).start()
 
-        @pl.when((n >= ADD_LAG) & (n < count + ADD_LAG))
-        def _():
-            m = n - ADD_LAG
-            left, right = pl.ds(0, wide // 2), pl.ds(wide // 2, wide // 2)
+        adding, m = at_step(i - ADD_LAG)
+
+        @pl.when(adding)
+        def _():
+            lo, hi = pl.ds(0, wide // 2), pl.ds(wide // 2, wide // 2)
             one(m, 0).wait_recv()
             one(m, 1).wait_recv()
             wider = jnp.float32
             second_out[m, 0] = (
-                part[m, 1 - row, col, :, left].astype(wider)
+                part[m, 1 - row, col, :, lo].astype(wider)
                 + first_in[m, 0, 1 - row].astype(wider)
             ).astype(jnp.bfloat16)
             second_out[m, 1] = (
-                part[m, row, 1 - col, :, right].astype(wider)
+                part[m, row, 1 - col, :, hi].astype(wider)
                 + first_in[m, 1, 1 - col].astype(wider)
             ).astype(jnp.bfloat16)
             two(m, 0).start()
             two(m, 1).start()
-            keep[m, 0] = part[m, row, col, :, left].astype(wider) + first_in[
+            keep[m, 0] = part[m, row, col, :, lo].astype(wider) + first_in[
                 m, 0, row
             ].astype(wider)
-            keep[m, 1] = part[m, row, col, :, right].astype(wider) + first_in[
+            keep[m, 1] = part[m, row, col, :, hi].astype(wider) + first_in[
                 m, 1, col
             ].astype(wider)
 
-        @pl.when(n >= END_LAG)
-        def _():
-            m = n - END_LAG
-            task, h, _, _ = piece(m)
-            two(m, 0).wait_recv()
-            two(m, 1).wait_recv()
-            rows = pl.ds(pl.multiple_of(task * LANES, LANES), LANES)
+        ending, e = at_step(i - END_LAG)
+
+        @pl.when(ending)
+        def _():
+            task, h, _, _ = piece(e)
+            two(e, 0).wait_recv()
+            two(e, 1).wait_recv()
+            at_rows = pl.ds(pl.multiple_of(task * LANES, LANES), LANES)
             for side in range(2):
                 at = pl.ds(pl.multiple_of(h * wide + side * (wide // 2), LANES), wide // 2)
-                total = keep[m, side] + second_in[m, side].astype(jnp.float32)
-                out[rows, at] = total.astype(jnp.bfloat16)
-
-    @pl.loop(0, count)
-    def _(n):
-        for side in range(2):
-            one(n, side).wait_send()
-            two(n, side).wait_send()
-
-    for h in range(CUTS):
-        to_mate(place, h).wait_send()
-        to_mate(place + 1, h).wait_send()
-        to_mate(3, h).wait_send()
-
-    @pl.when(outer)
-    def _():
-        for h in range(CUTS):
-            give(h).wait_send()
-            along(0, h, x.at[0, core, :, columns(h)], near).wait_send()
-
-    @pl.when(inner)
-    def _():
-        for h in range(CUTS):
-            along(1, h, x.at[1, core, :, columns(h)], near).wait_send()
-            along(2, h, other.at[:, columns(h)], facing).wait_send()
-            along(3, h, x.at[3, core, :, columns(h)], near).wait_send()
-            onward(h).wait_send()
-            to_mate(0, h).wait_send()
-
-
-def newton_kernel(
-    tok, blk, tokens, mine, kept, came, g, mixed, square, left, inverse, sent,
-    send_sem, recv_sem, pass_send, pass_recv, local_sem, out_sem, in_sem,
-):
-    t = lax.axis_index("tok")
-    b = lax.axis_index("blk")
-    low = b < blk // 2
+                total = keep[e, side] + second_in[e, side].astype(jnp.float32)
+                g[me, at_rows, at] = total.astype(jnp.bfloat16)
+
+    for s in range(stages):
+        every(1, 0, s)
+    for j in range(2):
+        hand(1, j, 0, True).start()
+    every(0, 2, 2)
+    every(0, 3, 2)
+    landed(1, 1, (1, 2))
+    landed(1, 2, (2,))
+    landed(1, 3, (2,))
+    for steps in range(4, 8):
+        landed(0, steps)
+    for steps in range(4, 8):
+        landed(1, steps)
+
+    for q in range(2):
+        for j in range(2):
+            for steps in range(2**stages):
+                hand(q, j, steps, False).wait_recv()
+
     half = blk // 2
     feats = g.shape[2]
-    owners = g.shape[0]
     width = square.shape[1]
     labels = width // feats
     rows = LANES
     factor = 1.0 / (tokens * divisor)
     shift = damping / divisor
-    dims = [(2, 0), (4, 0), (0, 1)]
-    count = len(dims)
-
-    def owner(device):
-        tt, bb = device
-        place = jnp.where(low, bb, blk - 1 - bb)
-        return place * (owners // 2) + tt % 2 * (owners // 4) + tt // 2
-
-    height = mine.shape[0]
-    groups = cut(height, 16, 2)
-    parts = [[(o + a, n) for a, n in cut(size, 16, count)] for o, size in groups]
-
-    def flip(j, steps, tok_bits=0):
-        blk_bits = 0
-        for s in range(count):
-            if steps >> s & 1:
-                dt, db = dims[(j + s) % count]
-                tok_bits ^= dt
-                blk_bits ^= db
-        return jnp.bitwise_xor(t, tok_bits), jnp.bitwise_xor(b, blk_bits)
-
-    def spot(q, j, device):
-        o, n = parts[q][j]
-        return g.at[owner(device), pl.ds(o, n)]
-
-    def own(q, j):
-        o, n = parts[q][j]
-        return mine.at[pl.ds(o, n)]
-
-    def slot(q, j, steps):
-        return (q * count + j) * 2**count + steps
-
-    def hop(q, j, steps, s):
-        index = slot(q, j, steps | 1 << s)
-        where = spot(q, j, flip(j, steps))
-        src = own(q, j) if steps == 0 else where
-        return remote(src, where, send_sem.at[index], recv_sem.at[index], flip(j, 1 << s))
-
-    def arrival(q, j, steps):
-        index = slot(q, j, steps)
-        where = spot(q, j, flip(j, steps))
-        return remote(where, where, send_sem.at[index], recv_sem.at[index], flip(j, 1))
-
-    mate = (jnp.bitwise_xor(t, 1), b)
-    across = (t, jnp.bitwise_xor(b, half))
-
-    def handed(q, j, steps, sender):
-        index = slot(q, j, steps)
-        where = spot(q, j, flip(j, steps, 0 if sender else 1))
-        src = own(q, j) if sender and steps == 0 else where
-        return remote(src, where, pass_send.at[index], pass_recv.at[index], mate)
-
-    meet([flip(0, 1 << s) for s in range(count)] + [mate, across])
-    pending = []
-
-    def start(copy):
-        copy.start()
-        pending.append(copy)
-
-    def begin(q):
-        for s in range(count):
-            for j in range(count):
-                start(hop(q, j, 0, s))
-        for j in range(count):
-            start(handed(q, j, 0, True))
-
-    def advance(q, p):
-        for steps in range(2**p, 2 ** (p + 1)):
-            for j in range(count):
-                arrival(q, j, steps).wait_recv()
-                for s in range(p + 1, count):
-                    start(hop(q, j, steps, s))
-                start(handed(q, j, steps, True))
-
-    begin(0)
-    local = pltpu.make_async_copy(mine, g.at[owner((t, b))], local_sem)
-    local.start()
-    for p in range(count - 1):
-        advance(0, p)
-    begin(1)
-    advance(0, count - 1)
-    for p in range(count):
-        advance(1, p)
-    local.wait()
-    for q in range(len(groups)):
-        for j in range(count):
-            for steps in range(2**count):
-                handed(q, j, steps, False).wait_recv()
-
     eye = lax.broadcasted_iota(jnp.int32, (LANES, LANES), 0) == lax.broadcasted_iota(
         jnp.int32, (LANES, LANES), 1
     )
-    eighth = owners // 2
 
     def diagonal(o, k, sub, axis):
         at = pl.ds(pl.multiple_of(sub * LANES, LANES), LANES)
@@ -468,12 +447,12 @@
         return lax.rsqrt(total / tokens + epsilon)
 
     for label in range(labels):
-        place, k = DIRECT[label, label]
+        plane, k = DIRECT[label, label]
 
         @pl.loop(0, eighth)
         def _(sub):
             at = pl.ds(pl.multiple_of(label * feats + sub * LANES, LANES), LANES)
-            inverse[:, at] = diagonal(place * eighth + sub, k, sub, 0)
+            inverse[:, at] = diagonal(plane * eighth + sub, k, sub, 0)
 
     block_of_rows = t // 2
     row_label = jnp.where(low, block_of_rows, labels - 1 - block_of_rows)
@@ -492,13 +471,13 @@
                 cols = slice(j * feats, (j + 1) * feats)
                 for s, sub in enumerate(subs):
                     if (label, j) in DIRECT:
-                        place, k = DIRECT[label, j]
-                        value = g[place * eighth + sub, k * LANES : (k + 1) * LANES, :]
+                        plane, k = DIRECT[label, j]
+                        value = g[plane * eighth + sub, k * LANES : (k + 1) * LANES, :]
                     else:
-                        place, k = DIRECT[j, label]
+                        plane, k = DIRECT[j, label]
                         at = pl.ds(pl.multiple_of(sub * LANES, LANES), LANES)
                         value = g[
-                            place * eighth : (place + 1) * eighth, k * LANES : (k + 1) * LANES, at
+                            plane * eighth : (plane + 1) * eighth, k * LANES : (k + 1) * LANES, at
                         ]
                         value = value.reshape(feats, LANES).T
                     mixed[s * rows : (s + 1) * rows, cols] = value
@@ -524,18 +503,18 @@
         for k in range(labels):
             lhs = left[:, k * feats : (k + 1) * feats]
             if (k, label) in DIRECT:
-                place, task = DIRECT[k, label]
+                plane, task = DIRECT[k, label]
                 rhs = g[
-                    place * eighth : (place + 1) * eighth,
+                    plane * eighth : (plane + 1) * eighth,
                     task * LANES : (task + 1) * LANES,
                     pl.ds(pl.multiple_of(h * step, LANES), step),
                 ].reshape(feats, step)
                 product = jnp.dot(lhs, rhs, preferred_element_type=jnp.float32)
             else:
-                place, task = DIRECT[label, k]
+                plane, task = DIRECT[label, k]
                 few = step // LANES
                 rhs = g[
-                    pl.ds(place * eighth + h * few, few), task * LANES : (task + 1) * LANES, :
+                    pl.ds(plane * eighth + h * few, few), task * LANES : (task + 1) * LANES, :
                 ].reshape(step, feats)
                 product = lax.dot_general(
                     lhs, rhs, (((1,), (1,)), ((), ())), preferred_element_type=jnp.float32
@@ -598,8 +577,38 @@
             copy.wait_recv()
             copy.wait_send()
 
-    for copy in pending:
-        copy.wait_send()
+    @pl.loop(0, count)
+    def _(n):
+        for side in range(2):
+            one(n, side).wait_send()
+            two(n, side).wait_send()
+
+    for h in range(CUTS):
+        to_mate(place, h).wait_send()
+        to_mate(place + 1, h).wait_send()
+        to_mate(3, h).wait_send()
+
+    @pl.when(outer)
+    def _():
+        for h in range(CUTS):
+            give(h).wait_send()
+            along(0, h, x.at[0, core, :, columns(h)], near).wait_send()
+
+    @pl.when(inner)
+    def _():
+        for h in range(CUTS):
+            along(1, h, x.at[1, core, :, columns(h)], near).wait_send()
+            along(2, h, other.at[:, columns(h)], facing).wait_send()
+            along(3, h, x.at[3, core, :, columns(h)], near).wait_send()
+            onward(h).wait_send()
+            to_mate(0, h).wait_send()
+
+    for q in range(2):
+        for j in range(2):
+            for steps in range(2**stages):
+                hand(q, j, steps, True).wait_send()
+                if steps:
+                    arrival(q, j, steps).wait_send()
 
 
 def cut(length, unit, pieces):
@@ -616,7 +625,7 @@
         out_specs=[pl.BlockSpec(memory_space=pltpu.VMEM)] * len(outs),
         scratch_shapes=scratch,
         compiler_params=pltpu.CompilerParams(
-            collective_id=collective_id, has_side_effects=True, vmem_limit_bytes=60 * 1024 * 1024
+            collective_id=collective_id, has_side_effects=True, vmem_limit_bytes=63 * 1024 * 1024
         ),
     )(*operands)
 
@@ -631,9 +640,11 @@
     wide = feats // CUTS
     bf16, f32 = jnp.bfloat16, jnp.float32
     dma = pltpu.SemaphoreType.DMA
-    (mine,) = call(
-        functools.partial(gram_kernel, tok, blk),
-        [jax.ShapeDtypeStruct((TASKS * rows, feats), bf16)],
+    steps = blk * CUTS
+    slots = 2 * 2 * 8
+    kept, came = call(
+        functools.partial(factor_kernel, tok, blk, tokens),
+        [jax.ShapeDtypeStruct((rows, width), f32), jax.ShapeDtypeStruct((rows, width), bf16)],
         [
             pltpu.VMEM((blk, 2, depth, feats), bf16),
             pltpu.VMEM((depth, feats), bf16),
@@ -644,30 +655,21 @@
             pltpu.VMEM((count, 2, rows, wide // 2), bf16),
             pltpu.VMEM((count, 2, rows, wide // 2), bf16),
             pltpu.VMEM((count, 2, rows, wide // 2), f32),
-            dma((2,)),
-            dma((blk, CUTS)), dma((blk, CUTS)),
-            dma((CUTS,)), dma((CUTS,)),
-            dma((blk, CUTS)), dma((blk, CUTS)),
-            dma((count, 2)), dma((count, 2)), dma((count, 2)), dma((count, 2)),
-        ],
-        0, pl.ANY, activations, out_grads,
-    )
-    slots = 2 * 3 * 8
-    steps = blk * CUTS
-    kept, came = call(
-        functools.partial(newton_kernel, tok, blk, tokens),
-        [jax.ShapeDtypeStruct((rows, width), f32), jax.ShapeDtypeStruct((rows, width), bf16)],
-        [
             pltpu.VMEM((2 * tok, TASKS * rows, feats), bf16),
             pltpu.VMEM((2 * rows, width), bf16),
             pltpu.VMEM((2 * rows, width), f32),
             pltpu.VMEM((2 * rows, width), bf16),
             pltpu.VMEM((1, width), f32),
             pltpu.VMEM((rows, width), bf16),
-            dma((slots,)), dma((slots,)), dma((slots,)), dma((slots,)), dma,
+            dma((2,)),
+            dma((blk, CUTS)), dma((blk, CUTS)),
+            dma((CUTS,)), dma((CUTS,)),
+            dma((blk, CUTS)), dma((blk, CUTS)),
+            dma((count, 2)), dma((count, 2)), dma((count, 2)), dma((count, 2)),
+            dma((slots,)), dma((slots,)), dma((slots,)), dma((slots,)),
             dma((steps,)), dma((steps,)),
         ],
-        1, pltpu.VMEM, mine,
+        0, pl.ANY, activations, out_grads,
     )
     came = came.astype(f32)
     return jnp.where(low, kept, came), jnp.where(low, came, kept)

time: 228 us -> 213 us (0.934)
  Pallas kernels: 223 us -> 207 us
    pallas_call x2 -> x1, Pallas kernels: 223 us -> 207 us  [call(): pl.pallas_call(kernel, out_shape=outs, in_specs=[pl.BlockSpec(memory_spac...]
where the time goes in v3:
time: 213 us; the launch traced here: 212 us
  Pallas kernels  207 us (97%)
  other arithmetic  4.38 us (2%)
    pallas_call x1, Pallas kernels, call(): pl.pallas_call(kernel, out_shape=outs, in_specs=[pl.BlockSpec(memory_spac...  207 us
    select_n x1, other arithmetic, split_body(): return (jnp.where(low, kept, came), jnp.where(low, came, kept))  4.38 us

profile of v3, /device:TPU:1, one launch (start us, length us, event | category | flops | bytes accessed | tf_op | source)
XLA Modules:
  0.0 212.3 jit_solution(14999715663060198285)
XLA Ops:
  0.6 207.3 %shard_map.41 = (f32[128,4096]{1,0:T(8,128)}, bf16[128,4096]{1,0:T(8,128)(2,1)}) custom-call(bf16[512,1024]{1,0:T(8,128)(2,1)} %acts.1, bf16[512,1024]{1,0:T(8,128)(2,1)} %grads.1), custom_call_target="tpu_custom_call" | custom-call | tf_op jit(solution)/shard_map/pallas_call | solution.py:621
  208.0 4.4 %convert_select_fusion = (f32[128,4096]{1,0:T(8,128)}, f32[128,4096]{1,0:T(8,128)}) fusion(f32[128,4096]{1,0:T(8,128)} %get-tuple-element.4, bf16[128,4096]{1,0:T(8,128)(2,1)} %get-tuple-element.5, pred[]{:T(512)S(6)} %lt.3), kind=kLoop, calls=%fused_computation | loop fusion | flops 1572864 | bytes 7340033 | tf_op jit(solution)/shard_map/jit(_where)/select_n | solution.py:675

commit v4 on v3

--- a/solution.py
+++ b/solution.py
@@ -76,12 +76,13 @@
 
 
 DIRECT = {
-    (0, 0): (0, 0), (0, 1): (0, 1), (0, 3): (0, 2), (1, 3): (0, 3), (3, 3): (0, 4),
-    (1, 1): (1, 0), (1, 2): (1, 1), (2, 0): (1, 2), (2, 3): (1, 3), (2, 2): (1, 4),
+    (0, 1): (0, 0), (0, 3): (0, 1), (1, 3): (0, 2),
+    (1, 2): (1, 0), (2, 0): (1, 1), (2, 3): (1, 2),
 }
-TASKS = 5
-EARLY = 2
+DIAGONAL = [(0, 0), (1, 0), (1, 1), (0, 1)]
 CUTS = 4
+SHORT = 3
+COUNT = 2 * SHORT + 3 * CUTS
 ADD_LAG = 3
 END_LAG = 6
 
@@ -110,7 +111,7 @@
 def factor_kernel(
     tok, blk, tokens, acts, grads, kept, came,
     x, other, passed, turned, part, first_in, second_out, second_in, keep,
-    g, mixed, square, left, inverse, sent,
+    g, diag, mixed, square, left, inverse, sent,
     load_sem, near_send, near_recv, pass_send, pass_recv, core_send, core_recv,
     one_send, one_recv, two_send, two_recv,
     hop_send, hop_recv, hand_send, hand_recv, out_sem, in_sem,
@@ -131,7 +132,10 @@
     depth, feats = other.shape
     wide = feats // CUTS
     halfway = feats // 2
-    count = TASKS * CUTS
+    count = COUNT
+    first = SHORT
+    split = SHORT + CUTS
+    tail = split + 2 * CUTS
 
     def load(ref, dst, index):
         return pltpu.make_async_copy(ref, dst, load_sem.at[index])
@@ -203,11 +207,12 @@
             along(1, h, x.at[1, core, :, columns(h)], near).start()
             along(2, h, other.at[:, columns(h)], facing).start()
 
-    def turn(slot, label):
+    def turn(slot, label, side):
+        at = pl.ds(pl.multiple_of(side * halfway, LANES), halfway)
         for c in range(2):
             for r in range(0, depth, 256):
                 turned[slot, :, c * depth + r : c * depth + r + 256] = x[
-                    label, c, r : r + 256, pl.ds(pl.multiple_of(core * halfway, LANES), halfway)
+                    label, c, r : r + 256, at
                 ].T
 
     def share(label, h):
@@ -215,12 +220,24 @@
         to_mate(label, h).start()
 
     def piece(n):
-        paired = (n >= 2 * CUTS) & (n < 4 * CUTS)
-        task = jnp.where(paired, 2 + n % 2, jnp.where(n < 2 * CUTS, n // CUTS, 4))
-        h = jnp.where(paired, n // 2 - CUTS, n % CUTS)
+        task = jnp.where(
+            n < first, 0,
+            jnp.where(n < split, 1, jnp.where(n < tail, 2 + (n - split) % 2, 4)),
+        )
+        h = jnp.where(
+            n < first, n,
+            jnp.where(
+                n < split, n - first, jnp.where(n < tail, (n - split) // 2, n - tail)
+            ),
+        )
+        whole = (task > 0) & (task < 4)
         slot = jnp.where(outer, pick(task, [0, 0, 0, 1, 2]), pick(task, [0, 0, 1, 1, 1]))
         label = jnp.where(outer, pick(task, [0, 1, 3, 3, 3]), pick(task, [1, 2, 0, 3, 2]))
-        return task, h, slot, label
+        corner = jnp.logical_not(whole) & (h == 2)
+        slot = jnp.where(corner, 3, slot)
+        inside = core * (CUTS // 2) + h
+        at = jnp.where(whole, h, jnp.where(h == 2, CUTS // 2 + core, inside))
+        return task, h, slot, label, at, whole
 
     def one(n, side):
         if side == 0:
@@ -239,12 +256,16 @@
 
     owners = g.shape[0]
     eighth = owners // 2
-    orders = [[[0, 1, 2], [1, 0, 2]], [[2, 0, 1], [2, 1, 0]]]
+    early, late = [[0, 1, 2], [1, 0, 2]], [[2, 0, 1], [2, 1, 0]]
+    orders = [early, early, late, late]
+    groups = len(orders)
     moves = [(2, 0), (4, 0), (0, 1)]
     stages = len(moves)
     ranges = []
-    for first, last in ((0, EARLY), (EARLY, TASKS)):
-        ranges.append([(first * LANES + o, n) for o, n in cut((last - first) * LANES, 16, 2)])
+    for ref, at_row, size in (
+        (diag, 0, LANES), (g, 0, LANES), (g, LANES, 2 * LANES), (diag, LANES, LANES)
+    ):
+        ranges.append([(ref, at_row + o, n) for o, n in cut(size, 16, 2)])
 
     def owner(device):
         tt, bb = device
@@ -263,8 +284,8 @@
         return jnp.bitwise_xor(t, tok_bits), jnp.bitwise_xor(b, blk_bits)
 
     def spot(q, j, device):
-        o, n = ranges[q][j]
-        return g.at[owner(device), pl.ds(o, n)]
+        ref, o, n = ranges[q][j]
+        return ref.at[owner(device), pl.ds(o, n)]
 
     def index_of(q, j, steps):
         return (q * 2 + j) * 2**stages + steps
@@ -297,24 +318,46 @@
                 hop(q, j, steps, s).start()
             hand(q, j, steps, True).start()
 
+    def begin(q):
+        for s in range(stages):
+            every(q, 0, s)
+        for j in range(2):
+            hand(q, j, 0, True).start()
+
+    def forward(h):
+        arrived(3, h).wait_recv()
+        to_mate(3, h).start()
+
+        @pl.when(inner)
+        def _():
+            along(3, h, x.at[3, core, :, columns(h)], near).start()
+
     for h in range(CUTS):
         from_mate(place, h).wait_recv()
-    turn(0, place)
-
-    split = 2 * CUTS
+    turn(0, place, core)
+    turn(3, place, 0)
     gap = END_LAG
 
     def at_step(i):
-        inside = (i >= 0) & ((i < split) | ((i >= split + gap) & (i < count + gap)))
-        return inside, jnp.where(i < split, i, i - gap)
-
-    @pl.loop(0, count + gap + END_LAG)
+        n = jnp.where(i < first, i, jnp.where(i < split + gap, i - gap, i - 2 * gap))
+        low_part = (i >= 0) & (i < first)
+        mid_part = (i >= first + gap) & (i < split + gap)
+        return low_part | mid_part | ((i >= split + 2 * gap) & (i < count + 2 * gap)), n
+
+    @pl.loop(0, count + 2 * gap + END_LAG)
     def _(i):
         active, n = at_step(i)
 
-        @pl.when(active & (n >= CUTS) & (n < split))
-        def _():
-            h = n - CUTS
+        @pl.when(i == first + gap)
+        def _():
+            for s in (0, 1):
+                every(0, 0, s)
+            for j in range(2):
+                hand(0, j, 0, True).start()
+
+        @pl.when(active & (n >= first) & (n < split))
+        def _():
+            h = n - first
 
             @pl.when(inner)
             def _():
@@ -326,45 +369,67 @@
 
         @pl.when(i == split + gap)
         def _():
-            for s in (0, 1):
-                every(0, 0, s)
-            for j in range(2):
-                hand(0, j, 0, True).start()
-            turn(1, place + 1)
-
-        @pl.when(i == split + gap + CUTS)
-        def _():
             landed(0, 1, (1,))
-
-        @pl.when(i == split + gap + 2 * CUTS)
+            turn(1, place + 1, core)
+
+        @pl.when(inner & (i == split + gap + gap // 2))
+        def _():
+            forward(0)
+
+        @pl.when(i == split + 2 * gap)
         def _():
             landed(0, 2)
             landed(0, 3)
+            for s in (0, 1):
+                every(1, 0, s)
+            for j in range(2):
+                hand(1, j, 0, True).start()
+
+        @pl.when(i == split + 2 * gap + CUTS)
+        def _():
+            landed(1, 1, (1,))
+
+        @pl.when(i == tail + 2 * gap)
+        def _():
             every(0, 0, 2)
             every(0, 1, 2)
 
-        @pl.when(active & (n >= split) & (n < 2 * split) & (n % 2 == 0))
-        def _():
-            h = n // 2 - CUTS
-            arrived(3, h).wait_recv()
-            to_mate(3, h).start()
+        @pl.when(i == tail + 2 * gap + SHORT)
+        def _():
+            landed(1, 2)
+            landed(1, 3)
+
+        @pl.when(i == tail + 2 * gap + END_LAG)
+        def _():
+            begin(2)
+
+        @pl.when(active & (n >= split) & (n < tail) & ((n - split) % 2 == 0))
+        def _():
+            h = (n - split) // 2
+
+            @pl.when(outer | (h > 0))
+            def _():
+                forward(h)
 
             @pl.when(inner)
             def _():
-                along(3, h, x.at[3, core, :, columns(h)], near).start()
                 share(0, h)
                 from_mate(0, h).wait_recv()
 
             from_mate(3, h).wait_recv()
 
-        @pl.when(outer & (i == 2 * split + gap))
-        def _():
-            turn(2, 3)
+        @pl.when(i == tail + 2 * gap)
+        def _():
+            turn(3, jnp.where(outer, 3, 2), 0)
+
+            @pl.when(outer)
+            def _():
+                turn(2, 3, core)
 
         @pl.when(active)
         def _():
-            task, h, slot, label = piece(n)
-            at = pl.ds(pl.multiple_of(h * wide, LANES), wide)
+            task, h, slot, label, cut_at, _ = piece(n)
+            at = pl.ds(pl.multiple_of(cut_at * wide, LANES), wide)
             right = x[label, :, :, at].reshape(2 * depth, wide)
             product = jnp.dot(turned[slot], right, preferred_element_type=jnp.float32)
             part[n] = product.astype(jnp.bfloat16).reshape(2, 2, LANES, wide)
@@ -400,36 +465,29 @@
 
         @pl.when(ending)
         def _():
-            task, h, _, _ = piece(e)
+            task, h, _, _, _, whole = piece(e)
             two(e, 0).wait_recv()
             two(e, 1).wait_recv()
-            at_rows = pl.ds(pl.multiple_of(task * LANES, LANES), LANES)
             for side in range(2):
                 at = pl.ds(pl.multiple_of(h * wide + side * (wide // 2), LANES), wide // 2)
                 total = keep[e, side] + second_in[e, side].astype(jnp.float32)
-                g[me, at_rows, at] = total.astype(jnp.bfloat16)
-
-    for s in range(stages):
-        every(1, 0, s)
-    for j in range(2):
-        hand(1, j, 0, True).start()
-    every(0, 2, 2)
-    every(0, 3, 2)
-    landed(1, 1, (1, 2))
-    landed(1, 2, (2,))
-    landed(1, 3, (2,))
-    for steps in range(4, 8):
-        landed(0, steps)
-    for steps in range(4, 8):
-        landed(1, steps)
-
-    for q in range(2):
+                total = total.astype(jnp.bfloat16)
+
+                @pl.when(whole)
+                def _():
+                    g[me, pl.ds(pl.multiple_of((task - 1) * LANES, LANES), LANES), at] = total
+
+                @pl.when(jnp.logical_not(whole))
+                def _():
+                    g_row = pl.multiple_of(task // 4 * LANES, LANES)
+                    diag[me, pl.ds(g_row, LANES), at] = total
+
+    def received(q):
         for j in range(2):
             for steps in range(2**stages):
                 hand(q, j, steps, False).wait_recv()
 
     half = blk // 2
-    feats = g.shape[2]
     width = square.shape[1]
     labels = width // feats
     rows = LANES
@@ -438,29 +496,85 @@
     eye = lax.broadcasted_iota(jnp.int32, (LANES, LANES), 0) == lax.broadcasted_iota(
         jnp.int32, (LANES, LANES), 1
     )
-
-    def diagonal(o, k, sub, axis):
-        at = pl.ds(pl.multiple_of(sub * LANES, LANES), LANES)
+    quarter = eighth // 2
+
+    def diagonal(plane, k, sub, axis):
+        at = pl.ds(pl.multiple_of(sub % quarter * LANES, LANES), LANES)
         own_rows = pl.ds(pl.multiple_of(k * LANES, LANES), LANES)
-        block = jnp.where(eye, g[o, own_rows, at].astype(jnp.float32), 0.0)
+        block = jnp.where(eye, diag[plane * eighth + sub, own_rows, at].astype(jnp.float32), 0.0)
         total = jnp.sum(block, axis=axis, keepdims=True)
         return lax.rsqrt(total / tokens + epsilon)
 
-    for label in range(labels):
-        plane, k = DIRECT[label, label]
-
-        @pl.loop(0, eighth)
-        def _(sub):
-            at = pl.ds(pl.multiple_of(label * feats + sub * LANES, LANES), LANES)
-            inverse[:, at] = diagonal(plane * eighth + sub, k, sub, 0)
+    def rebuild(which):
+        for label in range(labels):
+            plane, k = DIAGONAL[label]
+            if k != which:
+                continue
+
+            @pl.loop(0, eighth)
+            def _(sub):
+                at = pl.ds(pl.multiple_of(label * feats + sub * LANES, LANES), LANES)
+                inverse[:, at] = diagonal(plane, k, sub, 0)
+
+            own_rows = slice(k * LANES, (k + 1) * LANES)
+            ends = [
+                slice(plane * eighth + c * quarter, plane * eighth + (c + 1) * quarter)
+                for c in range(2)
+            ]
+            for c in range(2):
+                block = diag[ends[c], own_rows, :halfway].reshape(halfway, halfway)
+                x[label, c, :, c * halfway : (c + 1) * halfway] = block
+                lo = halfway + c * wide
+                block = diag[ends[c], own_rows, halfway : halfway + wide].reshape(halfway, wide)
+                x[label, 0, :, lo : lo + wide] = block
+                x[label, 1, c * wide : (c + 1) * wide, :halfway] = block.T
+
+    begin(3)
+    every(0, 2, 2)
+    every(0, 3, 2)
+    for steps in range(4):
+        every(1, steps, 2)
+    for h in range(CUTS):
+        to_mate(place, h).wait_send()
+        to_mate(place + 1, h).wait_send()
+        to_mate(3, h).wait_send()
+
+    @pl.when(outer)
+    def _():
+        for h in range(CUTS):
+            give(h).wait_send()
+            along(0, h, x.at[0, core, :, columns(h)], near).wait_send()
+
+    @pl.when(inner)
+    def _():
+        for h in range(CUTS):
+            along(1, h, x.at[1, core, :, columns(h)], near).wait_send()
+            along(2, h, other.at[:, columns(h)], facing).wait_send()
+            along(3, h, x.at[3, core, :, columns(h)], near).wait_send()
+            onward(h).wait_send()
+            to_mate(0, h).wait_send()
+
+    for q in (2, 3):
+        landed(q, 1, (1, 2))
+        landed(q, 2, (2,))
+        landed(q, 3, (2,))
+    for q in range(groups):
+        for steps in range(4, 8):
+            landed(q, steps)
+        if q == 0:
+            received(0)
+            rebuild(0)
+    for q in range(1, groups):
+        received(q)
+    rebuild(1)
 
     block_of_rows = t // 2
     row_label = jnp.where(low, block_of_rows, labels - 1 - block_of_rows)
     subs = [t % 2 * blk + bb for bb in (b, jnp.bitwise_xor(b, half))]
-    diag_place = pick(row_label, [DIRECT[i, i][0] for i in range(labels)])
-    diag_task = pick(row_label, [DIRECT[i, i][1] for i in range(labels)])
+    diag_plane = pick(row_label, [d[0] for d in DIAGONAL])
+    diag_task = pick(row_label, [d[1] for d in DIAGONAL])
     inverse_rows = jnp.concatenate(
-        [diagonal(diag_place * eighth + sub, diag_task, sub, 1) for sub in subs], axis=0
+        [diagonal(diag_plane, diag_task, sub, 1) for sub in subs], axis=0
     )
 
     for label in range(labels):
@@ -470,7 +584,10 @@
             for j in range(labels):
                 cols = slice(j * feats, (j + 1) * feats)
                 for s, sub in enumerate(subs):
-                    if (label, j) in DIRECT:
+                    if label == j:
+                        at = pl.ds(pl.multiple_of(sub % quarter * LANES, LANES), LANES)
+                        value = x[label, core, at, :]
+                    elif (label, j) in DIRECT:
                         plane, k = DIRECT[label, j]
                         value = g[plane * eighth + sub, k * LANES : (k + 1) * LANES, :]
                     else:
@@ -502,7 +619,11 @@
         total = None
         for k in range(labels):
             lhs = left[:, k * feats : (k + 1) * feats]
-            if (k, label) in DIRECT:
+            if k == label:
+                at = pl.ds(pl.multiple_of(h * step, LANES), step)
+                rhs = x[label, :, :, at].reshape(feats, step)
+                product = jnp.dot(lhs, rhs, preferred_element_type=jnp.float32)
+            elif (k, label) in DIRECT:
                 plane, task = DIRECT[k, label]
                 rhs = g[
                     plane * eighth : (plane + 1) * eighth,
@@ -569,6 +690,19 @@
             sent[:, to] = result[rows:].astype(jnp.bfloat16)
             copy.start()
 
+    @pl.loop(0, count)
+    def _(n):
+        for side in range(2):
+            one(n, side).wait_send()
+            two(n, side).wait_send()
+
+    for q in range(groups):
+        for j in range(2):
+            for steps in range(2**stages):
+                hand(q, j, steps, True).wait_send()
+                if steps:
+                    arrival(q, j, steps).wait_send()
+
     for label in range(labels):
 
         @pl.loop(0, CUTS)
@@ -576,39 +710,6 @@
             _, copy = swap(label, h)
             copy.wait_recv()
             copy.wait_send()
-
-    @pl.loop(0, count)
-    def _(n):
-        for side in range(2):
-            one(n, side).wait_send()
-            two(n, side).wait_send()
-
-    for h in range(CUTS):
-        to_mate(place, h).wait_send()
-        to_mate(place + 1, h).wait_send()
-        to_mate(3, h).wait_send()
-
-    @pl.when(outer)
-    def _():
-        for h in range(CUTS):
-            give(h).wait_send()
-            along(0, h, x.at[0, core, :, columns(h)], near).wait_send()
-
-    @pl.when(inner)
-    def _():
-        for h in range(CUTS):
-            along(1, h, x.at[1, core, :, columns(h)], near).wait_send()
-            along(2, h, other.at[:, columns(h)], facing).wait_send()
-            along(3, h, x.at[3, core, :, columns(h)], near).wait_send()
-            onward(h).wait_send()
-            to_mate(0, h).wait_send()
-
-    for q in range(2):
-        for j in range(2):
-            for steps in range(2**stages):
-                hand(q, j, steps, True).wait_send()
-                if steps:
-                    arrival(q, j, steps).wait_send()
 
 
 def cut(length, unit, pieces):
@@ -636,12 +737,12 @@
     width = feats * blk
     rows = width // (tok * blk)
     low = lax.axis_index("blk") < blk // 2
-    count = TASKS * CUTS
+    count = COUNT
     wide = feats // CUTS
     bf16, f32 = jnp.bfloat16, jnp.float32
     dma = pltpu.SemaphoreType.DMA
     steps = blk * CUTS
-    slots = 2 * 2 * 8
+    slots = 4 * 2 * 8
     kept, came = call(
         functools.partial(factor_kernel, tok, blk, tokens),
         [jax.ShapeDtypeStruct((rows, width), f32), jax.ShapeDtypeStruct((rows, width), bf16)],
@@ -649,13 +750,14 @@
             pltpu.VMEM((blk, 2, depth, feats), bf16),
             pltpu.VMEM((depth, feats), bf16),
             pltpu.VMEM((depth, feats), bf16),
-            pltpu.VMEM((3, feats // 2, 2 * depth), bf16),
+            pltpu.VMEM((4, feats // 2, 2 * depth), bf16),
             pltpu.VMEM((count, 2, 2, rows, wide), bf16),
             pltpu.VMEM((count, 2, 2, rows, wide // 2), bf16),
             pltpu.VMEM((count, 2, rows, wide // 2), bf16),
             pltpu.VMEM((count, 2, rows, wide // 2), bf16),
             pltpu.VMEM((count, 2, rows, wide // 2), f32),
-            pltpu.VMEM((2 * tok, TASKS * rows, feats), bf16),
+            pltpu.VMEM((2 * tok, 3 * rows, feats), bf16),
+            pltpu.VMEM((2 * tok, 2 * rows, feats // CUTS * SHORT), bf16),
             pltpu.VMEM((2 * rows, width), bf16),
             pltpu.VMEM((2 * rows, width), f32),
             pltpu.VMEM((2 * rows, width), bf16),
@@ -682,7 +784,7 @@
     def body(activations, out_grads):
         depth, feats = activations.shape
         whole = max(depth * tok, feats * blk) * feats * blk * activations.dtype.itemsize
-        cube = tok == 2 * blk and blk == 4 and feats == tok * LANES
+        cube = tok == 2 * blk and blk == 4 and feats == tok * LANES == 2 * depth
         if whole <= gathered_budget and cube:
             return split_body(tok, blk, activations, out_grads)
         return tiled_body(activations, out_grads)

time: 213 us -> 204 us (0.958)
  Pallas kernels: 207 us -> 199 us
    pallas_call x1, Pallas kernels: 207 us -> 199 us  [call(): pl.pallas_call(kernel, out_shape=outs, in_specs=[pl.BlockSpec(memory_spac...]
where the time goes in v4:
time: 204 us
  Pallas kernels  199 us (98%)
  other arithmetic  4.38 us (2%)
    pallas_call x1, Pallas kernels, call(): pl.pallas_call(kernel, out_shape=outs, in_specs=[pl.BlockSpec(memory_spac...  199 us
    select_n x1, other arithmetic, split_body(): return (jnp.where(low, kept, came), jnp.where(low, came, kept))  4.38 us

profile of v4, /device:TPU:1, one launch (start us, length us, event | category | flops | bytes accessed | tf_op | source)
XLA Modules:
  0.0 204.2 jit_solution(10194507125672326242)
XLA Ops:
  0.6 199.2 %shard_map.41 = (f32[128,4096]{1,0:T(8,128)}, bf16[128,4096]{1,0:T(8,128)(2,1)}) custom-call(bf16[512,1024]{1,0:T(8,128)(2,1)} %acts.1, bf16[512,1024]{1,0:T(8,128)(2,1)} %grads.1), custom_call_target="tpu_custom_call" | custom-call | tf_op jit(solution)/shard_map/pallas_call | solution.py:722
  199.8 4.4 %convert_select_fusion = (f32[128,4096]{1,0:T(8,128)}, f32[128,4096]{1,0:T(8,128)}) fusion(f32[128,4096]{1,0:T(8,128)} %get-tuple-element.4, bf16[128,4096]{1,0:T(8,128)(2,1)} %get-tuple-element.5, pred[]{:T(512)S(6)} %lt.3), kind=kLoop, calls=%fused_computation | loop fusion | flops 1572864 | bytes 7340033 | tf_op jit(solution)/shard_map/jit(_where)/select_n | solution.py:777

commit v5 on v4

--- a/solution.py
+++ b/solution.py
@@ -85,6 +85,7 @@
 COUNT = 2 * SHORT + 3 * CUTS
 ADD_LAG = 3
 END_LAG = 6
+STEPS = 2
 
 
 def pick(index, values):
@@ -109,12 +110,12 @@
 
 
 def factor_kernel(
-    tok, blk, tokens, acts, grads, kept, came,
+    tok, blk, tokens, acts, grads, act_out, grad_out,
     x, other, passed, turned, part, first_in, second_out, second_in, keep,
-    g, diag, mixed, square, left, inverse, sent,
+    g, diag, mixed, square, left, cubing, inverse, sent, kept, came, wider_in,
     load_sem, near_send, near_recv, pass_send, pass_recv, core_send, core_recv,
     one_send, one_recv, two_send, two_recv,
-    hop_send, hop_recv, hand_send, hand_recv, out_sem, in_sem,
+    hop_send, hop_recv, hand_send, hand_recv, out_sem, in_sem, kept_sem, came_sem,
 ):
     t = lax.axis_index("tok")
     b = lax.axis_index("blk")
@@ -369,7 +370,8 @@
 
         @pl.when(i == split + gap)
         def _():
-            landed(0, 1, (1,))
+            landed(0, 1, (1, 2))
+            every(0, 0, 2)
             turn(1, place + 1, core)
 
         @pl.when(inner & (i == split + gap + gap // 2))
@@ -391,8 +393,8 @@
 
         @pl.when(i == tail + 2 * gap)
         def _():
-            every(0, 0, 2)
-            every(0, 1, 2)
+            every(0, 2, 2)
+            every(0, 3, 2)
 
         @pl.when(i == tail + 2 * gap + SHORT)
         def _():
@@ -497,6 +499,7 @@
         jnp.int32, (LANES, LANES), 1
     )
     quarter = eighth // 2
+    step = feats // STEPS
 
     def diagonal(plane, k, sub, axis):
         at = pl.ds(pl.multiple_of(sub % quarter * LANES, LANES), LANES)
@@ -530,8 +533,6 @@
                 x[label, 1, c * wide : (c + 1) * wide, :halfway] = block.T
 
     begin(3)
-    every(0, 2, 2)
-    every(0, 3, 2)
     for steps in range(4):
         every(1, steps, 2)
     for h in range(CUTS):
@@ -554,16 +555,19 @@
             onward(h).wait_send()
             to_mate(0, h).wait_send()
 
-    for q in (2, 3):
-        landed(q, 1, (1, 2))
-        landed(q, 2, (2,))
-        landed(q, 3, (2,))
-    for q in range(groups):
+    landed(2, 1, (1, 2))
+    landed(2, 2, (2,))
+    for steps in range(4, 8):
+        landed(0, steps)
+    received(0)
+    rebuild(0)
+    landed(2, 3, (2,))
+    landed(3, 1, (1, 2))
+    landed(3, 2, (2,))
+    landed(3, 3, (2,))
+    for q in range(1, groups):
         for steps in range(4, 8):
             landed(q, steps)
-        if q == 0:
-            received(0)
-            rebuild(0)
     for q in range(1, groups):
         received(q)
     rebuild(1)
@@ -599,8 +603,8 @@
                         value = value.reshape(feats, LANES).T
                     mixed[s * rows : (s + 1) * rows, cols] = value
 
-    step = feats // CUTS
     starts = [row_label * feats + sub * LANES for sub in subs]
+    row_scale = factor * inverse_rows
 
     def identity(first_col, size):
         at = first_col + lax.broadcasted_iota(jnp.int32, (rows, size), 1)
@@ -609,16 +613,13 @@
             [(at - start == row).astype(jnp.float32) for start in starts], axis=0
         )
 
-    def scaled(first_col, size):
-        at = pl.ds(first_col, size)
-        return mixed[:, at].astype(jnp.float32) * (
-            factor * inverse_rows
-        ) * inverse[:, at] + shift * identity(first_col, size)
-
-    def fold(label, h):
+    def scaled(at):
+        return mixed[:, at].astype(jnp.float32) * row_scale * inverse[:, at]
+
+    def fold(lefts, label, h):
         total = None
         for k in range(labels):
-            lhs = left[:, k * feats : (k + 1) * feats]
+            lhs = lefts[:, k * feats : (k + 1) * feats]
             if k == label:
                 at = pl.ds(pl.multiple_of(h * step, LANES), step)
                 rhs = x[label, :, :, at].reshape(feats, step)
@@ -643,52 +644,61 @@
             total = product if total is None else total + product
         return total
 
-    @pl.loop(0, labels * CUTS)
+    @pl.loop(0, labels * STEPS)
     def _(i):
-        start_col = pl.multiple_of(i * step, step)
-        at = pl.ds(start_col, step)
-        left[:, at] = (scaled(start_col, step) * inverse[:, at]).astype(jnp.bfloat16)
+        at = pl.ds(pl.multiple_of(i * step, step), step)
+        left[:, at] = (scaled(at) * inverse[:, at]).astype(jnp.bfloat16)
 
     for label in range(labels):
 
-        @pl.loop(0, CUTS)
+        @pl.loop(0, STEPS)
+        def _(h):
+            at = pl.ds(pl.multiple_of(label * feats + h * step, step), step)
+            squared = fold(left, label, h) * (inverse[:, at] * factor)
+            square[:, at] = squared
+            cubing[:, at] = (squared * inverse[:, at]).astype(jnp.bfloat16)
+
+    def target(label, h):
+        to = jnp.where(low, label, labels - 1 - label)
+        return pl.ds(pl.multiple_of(to * feats + h * step, LANES), step), to * STEPS + h
+
+    def swap(label, h):
+        at, index = target(label, h)
+        return remote(
+            sent.at[:, at], came.at[:, at], out_sem.at[index], in_sem.at[index], across
+        )
+
+    def store(src, sems, label, h, out):
+        at, index = target(label, h)
+        return pltpu.make_async_copy(src.at[:, at], out.at[:, at], sems.at[index])
+
+    one_part = 4.0 - 6.0 * shift + 4.0 * shift**2 - shift**3
+    linear_part = -6.0 + 8.0 * shift - 3.0 * shift**2
+    square_part = 4.0 - 3.0 * shift
+
+    for label in range(labels):
+
+        @pl.loop(0, STEPS)
         def _(h):
             start_col = pl.multiple_of(label * feats + h * step, step)
             at = pl.ds(start_col, step)
-            square[:, at] = fold(label, h) * (inverse[:, at] * factor) + shift * scaled(
-                start_col, step
+            cube = fold(cubing, label, h) * (inverse[:, at] * factor)
+            result = (
+                one_part * identity(start_col, step) + linear_part * scaled(at)
+                + square_part * square[:, at] - cube
             )
-
-    @pl.loop(0, labels * CUTS)
-    def _(i):
-        start_col = pl.multiple_of(i * step, step)
-        at = pl.ds(start_col, step)
-        left[:, at] = (square[:, at] * inverse[:, at]).astype(jnp.bfloat16)
-
-    def swap(label, h):
-        to = jnp.where(low, label, labels - 1 - label)
-        at = pl.ds(pl.multiple_of(to * feats + h * step, LANES), step)
-        index = label * CUTS + h
-        return at, remote(
-            sent.at[:, at], came.at[:, at], out_sem.at[index], in_sem.at[index], across
-        )
-
-    for label in range(labels):
-
-        @pl.loop(0, CUTS)
-        def _(h):
-            start_col = pl.multiple_of(label * feats + h * step, step)
-            at = pl.ds(start_col, step)
-            squared = square[:, at]
-            cube = fold(label, h) * (inverse[:, at] * factor) + shift * squared
-            result = (
-                4.0 * identity(start_col, step) - 6.0 * scaled(start_col, step)
-                + 4.0 * squared - cube
-            )
-            to, copy = swap(label, h)
+            to, _ = target(label, h)
+            sent[:, to] = result[rows:].astype(jnp.bfloat16)
+            swap(label, h).start()
             kept[:, to] = result[:rows]
-            sent[:, to] = result[rows:].astype(jnp.bfloat16)
-            copy.start()
+
+            @pl.when(low)
+            def _():
+                store(kept, kept_sem, label, h, act_out).start()
+
+            @pl.when(jnp.logical_not(low))
+            def _():
+                store(kept, kept_sem, label, h, grad_out).start()
 
     @pl.loop(0, count)
     def _(n):
@@ -703,13 +713,28 @@
                 if steps:
                     arrival(q, j, steps).wait_send()
 
+    for label in reversed(range(labels)):
+
+        @pl.loop(0, STEPS)
+        def _(h):
+            to, _ = target(label, h)
+            swap(label, h).wait_recv()
+            wider_in[:, to] = came[:, to].astype(jnp.float32)
+
+            @pl.when(low)
+            def _():
+                store(wider_in, came_sem, label, h, grad_out).start()
+
+            @pl.when(jnp.logical_not(low))
+            def _():
+                store(wider_in, came_sem, label, h, act_out).start()
+
+            swap(label, h).wait_send()
+            store(kept, kept_sem, label, h, act_out).wait()
+
     for label in range(labels):
-
-        @pl.loop(0, CUTS)
-        def _(h):
-            _, copy = swap(label, h)
-            copy.wait_recv()
-            copy.wait_send()
+        for h in range(STEPS):
+            store(wider_in, came_sem, label, h, grad_out).wait()
 
 
 def cut(length, unit, pieces):
@@ -718,15 +743,15 @@
     return [(sum(sizes[:i]), sizes[i]) for i in range(pieces)]
 
 
-def call(kernel, outs, scratch, collective_id, space, *operands):
+def call(kernel, outs, scratch, *operands):
     return pl.pallas_call(
         kernel,
         out_shape=outs,
-        in_specs=[pl.BlockSpec(memory_space=space)] * len(operands),
-        out_specs=[pl.BlockSpec(memory_space=pltpu.VMEM)] * len(outs),
+        in_specs=[pl.BlockSpec(memory_space=pl.ANY)] * len(operands),
+        out_specs=[pl.BlockSpec(memory_space=pl.ANY)] * len(outs),
         scratch_shapes=scratch,
         compiler_params=pltpu.CompilerParams(
-            collective_id=collective_id, has_side_effects=True, vmem_limit_bytes=63 * 1024 * 1024
+            collective_id=0, has_side_effects=True, vmem_limit_bytes=63 * 1024 * 1024
         ),
     )(*operands)
 
@@ -736,16 +761,15 @@
     tokens = depth * tok
     width = feats * blk
     rows = width // (tok * blk)
-    low = lax.axis_index("blk") < blk // 2
     count = COUNT
     wide = feats // CUTS
     bf16, f32 = jnp.bfloat16, jnp.float32
     dma = pltpu.SemaphoreType.DMA
-    steps = blk * CUTS
+    steps = blk * STEPS
     slots = 4 * 2 * 8
-    kept, came = call(
+    return call(
         functools.partial(factor_kernel, tok, blk, tokens),
-        [jax.ShapeDtypeStruct((rows, width), f32), jax.ShapeDtypeStruct((rows, width), bf16)],
+        [jax.ShapeDtypeStruct((rows, width), f32)] * 2,
         [
             pltpu.VMEM((blk, 2, depth, feats), bf16),
             pltpu.VMEM((depth, feats), bf16),
@@ -761,20 +785,22 @@
             pltpu.VMEM((2 * rows, width), bf16),
             pltpu.VMEM((2 * rows, width), f32),
             pltpu.VMEM((2 * rows, width), bf16),
+            pltpu.VMEM((2 * rows, width), bf16),
             pltpu.VMEM((1, width), f32),
             pltpu.VMEM((rows, width), bf16),
+            pltpu.VMEM((rows, width), f32),
+            pltpu.VMEM((rows, width), bf16),
+            pltpu.VMEM((rows, width), f32),
             dma((2,)),
             dma((blk, CUTS)), dma((blk, CUTS)),
             dma((CUTS,)), dma((CUTS,)),
             dma((blk, CUTS)), dma((blk, CUTS)),
             dma((count, 2)), dma((count, 2)), dma((count, 2)), dma((count, 2)),
             dma((slots,)), dma((slots,)), dma((slots,)), dma((slots,)),
-            dma((steps,)), dma((steps,)),
+            dma((steps,)), dma((steps,)), dma((steps,)), dma((steps,)),
         ],
-        0, pl.ANY, activations, out_grads,
+        activations, out_grads,
     )
-    came = came.astype(f32)
-    return jnp.where(low, kept, came), jnp.where(low, came, kept)
 
 
 def solution(mesh):

time: 204 us -> 193 us (0.946)
  Pallas kernels: 199 us -> 187 us
  local copies, waits for them, and re-layouts: 0 us -> 4.58 us
  other arithmetic: 4.38 us -> 0 us
    pallas_call x1, Pallas kernels: 199 us -> 187 us  [call(): pl.pallas_call(kernel, out_shape=outs, in_specs=[pl.BlockSpec(memory_spac...]
    unnamed x0 -> x4, local copies, waits for them, and re-layouts: none -> 4.58 us
    select_n x1 -> x0, other arithmetic: 4.38 us -> none  [split_body(): return (jnp.where(low, kept, came), jnp.where(low, came, kept))]
where the time goes in v5:
time: 193 us
  Pallas kernels  187 us (97%)
  local copies, waits for them, and re-layouts  4.58 us (2%)
    pallas_call x1, Pallas kernels, call(): pl.pallas_call(kernel, out_shape=outs, in_specs=[pl.BlockSpec(memory_spac...  187 us
    unnamed x4, local copies, waits for them, and re-layouts  4.58 us

profile of v5, /device:TPU:1, one launch (start us, length us, event | category | flops | bytes accessed | tf_op | source)
XLA Modules:
  0.0 192.7 jit_solution(6038772316412766281)
XLA Ops:
  0.6 187.5 %shard_map.41 = (f32[128,4096]{1,0:T(8,128)}, f32[128,4096]{1,0:T(8,128)}) custom-call(bf16[512,1024]{1,0:T(8,128)(2,1)} %acts.1, bf16[512,1024]{1,0:T(8,128)(2,1)} %grads.1), custom_call_target="tpu_custom_call" | custom-call | tf_op jit(solution)/shard_map/pallas_call | solution.py:747
  188.1 0.0 copy-start
  188.1 3.3 %copy.6 = f32[128,4096]{1,0:T(8,128)} copy(f32[128,4096]{1,0:T(8,128)} %get-tuple-element.4) | data formatting | bytes 4194304
  191.4 0.0 copy-done
  191.4 1.3 copy.7
Async XLA Ops:
  188.1 3.3 %copy-start = (f32[128,4096]{1,0:T(8,128)S(1)}, f32[128,4096]{1,0:T(8,128)}, u32[]{:S(2)}) copy-start(f32[128,4096]{1,0:T(8,128)} %get-tuple-element.5) | copy-start | bytes 6291460

commit v6 on v5

--- a/solution.py
+++ b/solution.py
@@ -161,35 +161,35 @@
     def to_mate(label, h):
         here = x.at[label, core, :, columns(h)]
         return remote(
-            here, here, core_send.at[label, h], core_recv.at[label, h], mate
+            here, here, core_send, core_recv.at[label, h], mate
         )
 
     def from_mate(label, h):
         there = x.at[label, 1 - core, :, columns(h)]
         return remote(
-            there, there, core_send.at[label, h], core_recv.at[label, h], mate
+            there, there, core_send, core_recv.at[label, h], mate
         )
 
     def along(label, h, src, device):
         return remote(
             src, x.at[label, core, :, columns(h)],
-            near_send.at[label, h], near_recv.at[label, h], device,
+            near_send, near_recv.at[label, h], device,
         )
 
     def arrived(label, h):
         here = x.at[label, core, :, columns(h)]
-        return remote(here, here, near_send.at[label, h], near_recv.at[label, h], near)
+        return remote(here, here, near_send, near_recv.at[label, h], near)
 
     def give(h):
         return remote(
             other.at[:, columns(h)], passed.at[:, columns(h)],
-            pass_send.at[h], pass_recv.at[h], near,
+            pass_send, pass_recv.at[h], near,
         )
 
     def onward(h):
         return remote(
             passed.at[:, columns(h)], x.at[3, core, :, columns(h)],
-            pass_send.at[h], near_recv.at[3, h], facing,
+            pass_send, near_recv.at[3, h], facing,
         )
 
     for h in range(CUTS):
@@ -240,19 +240,25 @@
         at = jnp.where(whole, h, jnp.where(h == 2, CUTS // 2 + core, inside))
         return task, h, slot, label, at, whole
 
+    def both(ref, sem):
+        remote(ref, ref, sem, sem, mate).wait_recv()
+
+    def sent_all(ref, sem):
+        remote(ref, ref, sem, sem, mate).wait_send()
+
     def one(n, side):
         if side == 0:
             src, device = part.at[n, :, 1 - col, :, pl.ds(0, wide // 2)], beside
         else:
             src, device = part.at[n, 1 - row, :, :, pl.ds(wide // 2, wide // 2)], below
         return remote(
-            src, first_in.at[n, side], one_send.at[n, side], one_recv.at[n, side], device
+            src, first_in.at[n, side], one_send, one_recv.at[n], device
         )
 
     def two(n, side):
         return remote(
             second_out.at[n, side], second_in.at[n, side],
-            two_send.at[n, side], two_recv.at[n, side], below if side == 0 else beside,
+            two_send, two_recv.at[n], below if side == 0 else beside,
         )
 
     owners = g.shape[0]
@@ -288,42 +294,39 @@
         ref, o, n = ranges[q][j]
         return ref.at[owner(device), pl.ds(o, n)]
 
-    def index_of(q, j, steps):
-        return (q * 2 + j) * 2**stages + steps
+    kinds = [0, 1, 1, 0]
+
+    def whole_rows(q, owner_at):
+        ref, o, n = ranges[q][0]
+        return ref.at[owner_at, pl.ds(o, n + ranges[q][1][2])]
 
     def hop(q, j, steps, s):
-        index = index_of(q, j, steps | 1 << s)
         where = spot(q, j, flip(q, j, steps))
         return remote(
-            where, where, hop_send.at[index], hop_recv.at[index], flip(q, j, 1 << s)
-        )
-
-    def arrival(q, j, steps):
-        index = index_of(q, j, steps)
+            where, where, hop_send.at[kinds[q]], hop_recv.at[q, steps | 1 << s],
+            flip(q, j, 1 << s),
+        )
+
+    def hand(q, j, steps):
         where = spot(q, j, flip(q, j, steps))
-        return remote(where, where, hop_send.at[index], hop_recv.at[index], flip(q, j, 1))
-
-    def hand(q, j, steps, sender):
-        index = index_of(q, j, steps)
-        where = spot(q, j, flip(q, j, steps, 0 if sender else 1))
-        return remote(where, where, hand_send.at[index], hand_recv.at[index], mate)
+        return remote(where, where, hand_send.at[kinds[q]], hand_recv.at[q], mate)
 
     def every(q, steps, s):
         for j in range(2):
             hop(q, j, steps, s).start()
 
     def landed(q, steps, onward_to=()):
+        both(whole_rows(q, me), hop_recv.at[q, steps])
         for j in range(2):
-            arrival(q, j, steps).wait_recv()
             for s in onward_to:
                 hop(q, j, steps, s).start()
-            hand(q, j, steps, True).start()
+            hand(q, j, steps).start()
 
     def begin(q):
         for s in range(stages):
             every(q, 0, s)
         for j in range(2):
-            hand(q, j, 0, True).start()
+            hand(q, j, 0).start()
 
     def forward(h):
         arrived(3, h).wait_recv()
@@ -354,7 +357,7 @@
             for s in (0, 1):
                 every(0, 0, s)
             for j in range(2):
-                hand(0, j, 0, True).start()
+                hand(0, j, 0).start()
 
         @pl.when(active & (n >= first) & (n < split))
         def _():
@@ -385,7 +388,7 @@
             for s in (0, 1):
                 every(1, 0, s)
             for j in range(2):
-                hand(1, j, 0, True).start()
+                hand(1, j, 0).start()
 
         @pl.when(i == split + 2 * gap + CUTS)
         def _():
@@ -443,8 +446,7 @@
         @pl.when(adding)
         def _():
             lo, hi = pl.ds(0, wide // 2), pl.ds(wide // 2, wide // 2)
-            one(m, 0).wait_recv()
-            one(m, 1).wait_recv()
+            both(first_in.at[m], one_recv.at[m])
             wider = jnp.float32
             second_out[m, 0] = (
                 part[m, 1 - row, col, :, lo].astype(wider)
@@ -468,8 +470,7 @@
         @pl.when(ending)
         def _():
             task, h, _, _, _, whole = piece(e)
-            two(e, 0).wait_recv()
-            two(e, 1).wait_recv()
+            both(second_in.at[e], two_recv.at[e])
             for side in range(2):
                 at = pl.ds(pl.multiple_of(h * wide + side * (wide // 2), LANES), wide // 2)
                 total = keep[e, side] + second_in[e, side].astype(jnp.float32)
@@ -485,9 +486,7 @@
                     diag[me, pl.ds(g_row, LANES), at] = total
 
     def received(q):
-        for j in range(2):
-            for steps in range(2**stages):
-                hand(q, j, steps, False).wait_recv()
+        both(whole_rows(q, pl.ds(0, 2**stages)), hand_recv.at[q])
 
     half = blk // 2
     width = square.shape[1]
@@ -535,25 +534,17 @@
     begin(3)
     for steps in range(4):
         every(1, steps, 2)
-    for h in range(CUTS):
-        to_mate(place, h).wait_send()
-        to_mate(place + 1, h).wait_send()
-        to_mate(3, h).wait_send()
+    sent_all(other, pass_send)
 
     @pl.when(outer)
     def _():
-        for h in range(CUTS):
-            give(h).wait_send()
-            along(0, h, x.at[0, core, :, columns(h)], near).wait_send()
+        sent_all(x.at[pl.ds(0, 3), 0], core_send)
+        sent_all(x.at[pl.ds(0, 1), 0], near_send)
 
     @pl.when(inner)
     def _():
-        for h in range(CUTS):
-            along(1, h, x.at[1, core, :, columns(h)], near).wait_send()
-            along(2, h, other.at[:, columns(h)], facing).wait_send()
-            along(3, h, x.at[3, core, :, columns(h)], near).wait_send()
-            onward(h).wait_send()
-            to_mate(0, h).wait_send()
+        sent_all(x.at[pl.ds(0, 4), 0], core_send)
+        sent_all(x.at[pl.ds(0, 3), 0], near_send)
 
     landed(2, 1, (1, 2))
     landed(2, 2, (2,))
@@ -665,12 +656,12 @@
     def swap(label, h):
         at, index = target(label, h)
         return remote(
-            sent.at[:, at], came.at[:, at], out_sem.at[index], in_sem.at[index], across
+            sent.at[:, at], came.at[:, at], out_sem, in_sem.at[index], across
         )
 
     def store(src, sems, label, h, out):
-        at, index = target(label, h)
-        return pltpu.make_async_copy(src.at[:, at], out.at[:, at], sems.at[index])
+        at, _ = target(label, h)
+        return pltpu.make_async_copy(src.at[:, at], out.at[:, at], sems)
 
     one_part = 4.0 - 6.0 * shift + 4.0 * shift**2 - shift**3
     linear_part = -6.0 + 8.0 * shift - 3.0 * shift**2
@@ -700,18 +691,11 @@
             def _():
                 store(kept, kept_sem, label, h, grad_out).start()
 
-    @pl.loop(0, count)
-    def _(n):
-        for side in range(2):
-            one(n, side).wait_send()
-            two(n, side).wait_send()
-
-    for q in range(groups):
-        for j in range(2):
-            for steps in range(2**stages):
-                hand(q, j, steps, True).wait_send()
-                if steps:
-                    arrival(q, j, steps).wait_send()
+    sent_all(first_in, one_send)
+    sent_all(second_in, two_send)
+    for kind, ref in enumerate((diag, g)):
+        sent_all(ref.at[pl.ds(0, 2**stages - 1)], hop_send.at[kind])
+        sent_all(ref.at[pl.ds(0, 2**stages)], hand_send.at[kind])
 
     for label in reversed(range(labels)):
 
@@ -729,12 +713,9 @@
             def _():
                 store(wider_in, came_sem, label, h, act_out).start()
 
-            swap(label, h).wait_send()
-            store(kept, kept_sem, label, h, act_out).wait()
-
-    for label in range(labels):
-        for h in range(STEPS):
-            store(wider_in, came_sem, label, h, grad_out).wait()
+    sent_all(sent, out_sem)
+    pltpu.make_async_copy(kept, act_out, kept_sem).wait()
+    pltpu.make_async_copy(wider_in, grad_out, came_sem).wait()
 
 
 def cut(length, unit, pieces):
@@ -766,7 +747,6 @@
     bf16, f32 = jnp.bfloat16, jnp.float32
     dma = pltpu.SemaphoreType.DMA
     steps = blk * STEPS
-    slots = 4 * 2 * 8
     return call(
         functools.partial(factor_kernel, tok, blk, tokens),
         [jax.ShapeDtypeStruct((rows, width), f32)] * 2,
@@ -792,12 +772,10 @@
             pltpu.VMEM((rows, width), bf16),
             pltpu.VMEM((rows, width), f32),
             dma((2,)),
-            dma((blk, CUTS)), dma((blk, CUTS)),
-            dma((CUTS,)), dma((CUTS,)),
-            dma((blk, CUTS)), dma((blk, CUTS)),
-            dma((count, 2)), dma((count, 2)), dma((count, 2)), dma((count, 2)),
-            dma((slots,)), dma((slots,)), dma((slots,)), dma((slots,)),
-            dma((steps,)), dma((steps,)), dma((steps,)), dma((steps,)),
+            dma, dma((blk, CUTS)), dma, dma((CUTS,)), dma, dma((blk, CUTS)),
+            dma, dma((count,)), dma, dma((count,)),
+            dma((2,)), dma((4, 8)), dma((2,)), dma((4,)),
+            dma, dma((steps,)), dma, dma,
         ],
         activations, out_grads,
     )

time: 193 us -> 191 us (0.990)
  Pallas kernels: 187 us -> 185 us
    pallas_call x1, Pallas kernels: 187 us -> 185 us  [call(): pl.pallas_call(kernel, out_shape=outs, in_specs=[pl.BlockSpec(memory_spac...]
where the time goes in v6:
time: 191 us; the launch traced here: 190 us
  Pallas kernels  185 us (97%)
  local copies, waits for them, and re-layouts  4.58 us (2%)
    pallas_call x1, Pallas kernels, call(): pl.pallas_call(kernel, out_shape=outs, in_specs=[pl.BlockSpec(memory_spac...  185 us
    unnamed x4, local copies, waits for them, and re-layouts  4.58 us

profile of v6, /device:TPU:1, one launch (start us, length us, event | category | flops | bytes accessed | tf_op | source)
XLA Modules:
  0.0 190.5 jit_solution(2942166125287768965)
XLA Ops:
  0.6 185.2 %shard_map.41 = (f32[128,4096]{1,0:T(8,128)}, f32[128,4096]{1,0:T(8,128)}) custom-call(bf16[512,1024]{1,0:T(8,128)(2,1)} %acts.1, bf16[512,1024]{1,0:T(8,128)(2,1)} %grads.1), custom_call_target="tpu_custom_call" | custom-call | tf_op jit(solution)/shard_map/pallas_call | solution.py:728
  185.9 0.0 copy-start
  185.9 3.3 %copy.6 = f32[128,4096]{1,0:T(8,128)} copy(f32[128,4096]{1,0:T(8,128)} %get-tuple-element.4) | data formatting | bytes 4194304
  189.1 0.0 copy-done
  189.2 1.3 copy.7
Async XLA Ops:
  185.9 3.3 %copy-start = (f32[128,4096]{1,0:T(8,128)S(1)}, f32[128,4096]{1,0:T(8,128)}, u32[]{:S(2)}) copy-start(f32[128,4096]{1,0:T(8,128)} %get-tuple-element.5) | copy-start | bytes 6291460

commit v7 on v6

--- a/solution.py
+++ b/solution.py
@@ -597,20 +597,22 @@
     starts = [row_label * feats + sub * LANES for sub in subs]
     row_scale = factor * inverse_rows
 
-    def identity(first_col, size):
+    def share_of(part):
+        return slice(part * rows, (part + 1) * rows)
+
+    def identity(part, first_col, size):
         at = first_col + lax.broadcasted_iota(jnp.int32, (rows, size), 1)
         row = lax.broadcasted_iota(jnp.int32, (rows, size), 0)
-        return jnp.concatenate(
-            [(at - start == row).astype(jnp.float32) for start in starts], axis=0
-        )
-
-    def scaled(at):
-        return mixed[:, at].astype(jnp.float32) * row_scale * inverse[:, at]
-
-    def fold(lefts, label, h):
+        return (at - starts[part] == row).astype(jnp.float32)
+
+    def scaled(part, at):
+        own_rows = share_of(part)
+        return mixed[own_rows, at].astype(jnp.float32) * row_scale[own_rows] * inverse[:, at]
+
+    def fold(lefts, part, label, h):
         total = None
         for k in range(labels):
-            lhs = lefts[:, k * feats : (k + 1) * feats]
+            lhs = lefts[share_of(part), k * feats : (k + 1) * feats]
             if k == label:
                 at = pl.ds(pl.multiple_of(h * step, LANES), step)
                 rhs = x[label, :, :, at].reshape(feats, step)
@@ -635,19 +637,22 @@
             total = product if total is None else total + product
         return total
 
-    @pl.loop(0, labels * STEPS)
-    def _(i):
-        at = pl.ds(pl.multiple_of(i * step, step), step)
-        left[:, at] = (scaled(at) * inverse[:, at]).astype(jnp.bfloat16)
-
-    for label in range(labels):
-
-        @pl.loop(0, STEPS)
-        def _(h):
-            at = pl.ds(pl.multiple_of(label * feats + h * step, step), step)
-            squared = fold(left, label, h) * (inverse[:, at] * factor)
-            square[:, at] = squared
-            cubing[:, at] = (squared * inverse[:, at]).astype(jnp.bfloat16)
+    def square_rows(part):
+        own_rows = share_of(part)
+
+        @pl.loop(0, labels * STEPS)
+        def _(i):
+            at = pl.ds(pl.multiple_of(i * step, step), step)
+            left[own_rows, at] = (scaled(part, at) * inverse[:, at]).astype(jnp.bfloat16)
+
+        for label in range(labels):
+
+            @pl.loop(0, STEPS)
+            def _(h):
+                at = pl.ds(pl.multiple_of(label * feats + h * step, step), step)
+                squared = fold(left, part, label, h) * (inverse[:, at] * factor)
+                square[own_rows, at] = squared
+                cubing[own_rows, at] = (squared * inverse[:, at]).astype(jnp.bfloat16)
 
     def target(label, h):
         to = jnp.where(low, label, labels - 1 - label)
@@ -667,21 +672,31 @@
     linear_part = -6.0 + 8.0 * shift - 3.0 * shift**2
     square_part = 4.0 - 3.0 * shift
 
+    def cube_chunk(part, label, h):
+        start_col = pl.multiple_of(label * feats + h * step, step)
+        at = pl.ds(start_col, step)
+        cube = fold(cubing, part, label, h) * (inverse[:, at] * factor)
+        return (
+            one_part * identity(part, start_col, step) + linear_part * scaled(part, at)
+            + square_part * square[share_of(part), at] - cube
+        )
+
+    square_rows(1)
     for label in range(labels):
 
         @pl.loop(0, STEPS)
         def _(h):
-            start_col = pl.multiple_of(label * feats + h * step, step)
-            at = pl.ds(start_col, step)
-            cube = fold(cubing, label, h) * (inverse[:, at] * factor)
-            result = (
-                one_part * identity(start_col, step) + linear_part * scaled(at)
-                + square_part * square[:, at] - cube
-            )
             to, _ = target(label, h)
-            sent[:, to] = result[rows:].astype(jnp.bfloat16)
+            sent[:, to] = cube_chunk(1, label, h).astype(jnp.bfloat16)
             swap(label, h).start()
-            kept[:, to] = result[:rows]
+
+    square_rows(0)
+    for label in range(labels):
+
+        @pl.loop(0, STEPS)
+        def _(h):
+            to, _ = target(label, h)
+            kept[:, to] = cube_chunk(0, label, h)
 
             @pl.when(low)
             def _():

time: 191 us -> 188 us (0.984)
  Pallas kernels: 185 us -> 183 us
    pallas_call x1, Pallas kernels: 185 us -> 183 us  [call(): pl.pallas_call(kernel, out_shape=outs, in_specs=[pl.BlockSpec(memory_spac...]
where the time goes in v7:
time: 188 us
  Pallas kernels  183 us (97%)
  local copies, waits for them, and re-layouts  4.58 us (2%)
    pallas_call x1, Pallas kernels, call(): pl.pallas_call(kernel, out_shape=outs, in_specs=[pl.BlockSpec(memory_spac...  183 us
    unnamed x4, local copies, waits for them, and re-layouts  4.58 us

profile of v7, /device:TPU:1, one launch (start us, length us, event | category | flops | bytes accessed | tf_op | source)
XLA Modules:
  0.0 188.1 jit_solution(8310741350684128853)
XLA Ops:
  0.6 182.9 %shard_map.41 = (f32[128,4096]{1,0:T(8,128)}, f32[128,4096]{1,0:T(8,128)}) custom-call(bf16[512,1024]{1,0:T(8,128)(2,1)} %acts.1, bf16[512,1024]{1,0:T(8,128)(2,1)} %grads.1), custom_call_target="tpu_custom_call" | custom-call | tf_op jit(solution)/shard_map/pallas_call | solution.py:743
  183.5 0.0 copy-start
  183.5 3.3 %copy.6 = f32[128,4096]{1,0:T(8,128)} copy(f32[128,4096]{1,0:T(8,128)} %get-tuple-element.4) | data formatting | bytes 4194304
  186.8 0.0 copy-done
  186.8 1.3 copy.7
Async XLA Ops:
  183.5 3.3 %copy-start = (f32[128,4096]{1,0:T(8,128)S(1)}, f32[128,4096]{1,0:T(8,128)}, u32[]{:S(2)}) copy-start(f32[128,4096]{1,0:T(8,128)} %get-tuple-element.5) | copy-start | bytes 6291460

commit v8 on v7

--- a/solution.py
+++ b/solution.py
@@ -387,6 +387,11 @@
             landed(0, 3)
             for s in (0, 1):
                 every(1, 0, s)
+
+            @pl.when(outer)
+            def _():
+                every(1, 0, 2)
+
             for j in range(2):
                 hand(1, j, 0).start()
 
@@ -532,7 +537,12 @@
                 x[label, 1, c * wide : (c + 1) * wide, :halfway] = block.T
 
     begin(3)
-    for steps in range(4):
+
+    @pl.when(inner)
+    def _():
+        every(1, 0, 2)
+
+    for steps in range(1, 4):
         every(1, steps, 2)
     sent_all(other, pass_send)
 
@@ -682,7 +692,7 @@
         )
 
     square_rows(1)
-    for label in range(labels):
+    for label in [labels - 1, *range(labels - 1)]:
 
         @pl.loop(0, STEPS)
         def _(h):
@@ -712,7 +722,7 @@
         sent_all(ref.at[pl.ds(0, 2**stages - 1)], hop_send.at[kind])
         sent_all(ref.at[pl.ds(0, 2**stages)], hand_send.at[kind])
 
-    for label in reversed(range(labels)):
+    for label in [0, *reversed(range(1, labels))]:
 
         @pl.loop(0, STEPS)
         def _(h):

time: 188 us -> 188 us (level)
  no operation moved by 1% of the time
where the time goes in v8:
time: 188 us
  Pallas kernels  182 us (97%)
  local copies, waits for them, and re-layouts  4.58 us (2%)
    pallas_call x1, Pallas kernels, call(): pl.pallas_call(kernel, out_shape=outs, in_specs=[pl.BlockSpec(memory_spac...  182 us
    unnamed x4, local copies, waits for them, and re-layouts  4.58 us

profile of v8, /device:TPU:1, one launch (start us, length us, event | category | flops | bytes accessed | tf_op | source)
XLA Modules:
  0.0 187.7 jit_solution(16166323312237433147)
XLA Ops:
  0.6 182.5 %shard_map.41 = (f32[128,4096]{1,0:T(8,128)}, f32[128,4096]{1,0:T(8,128)}) custom-call(bf16[512,1024]{1,0:T(8,128)(2,1)} %acts.1, bf16[512,1024]{1,0:T(8,128)(2,1)} %grads.1), custom_call_target="tpu_custom_call" | custom-call | tf_op jit(solution)/shard_map/pallas_call | solution.py:753
  183.1 0.0 copy-start
  183.1 3.3 %copy.6 = f32[128,4096]{1,0:T(8,128)} copy(f32[128,4096]{1,0:T(8,128)} %get-tuple-element.4) | data formatting | bytes 4194304
  186.4 0.0 copy-done
  186.4 1.3 copy.7
Async XLA Ops:
  183.1 3.3 %copy-start = (f32[128,4096]{1,0:T(8,128)S(1)}, f32[128,4096]{1,0:T(8,128)}, u32[]{:S(2)}) copy-start(f32[128,4096]{1,0:T(8,128)} %get-tuple-element.5) | copy-start | bytes 6291460
